TPU v7x, 32 devices: a whole 2x2x4 slice. The times are simulated.
32 devices in a mesh: lat: 4 (over y, x), lon: 8 (over z, core).
Axes of the slice: x: 2, y: 2, z: 4, core: 2. Of those that a mesh axis runs over, the one named last changes fastest.
Arguments:
- right_side: float32 [8, 768, 1024], P(None, 'lat', 'lon'), may hold values from -16 to 16
- center: float32 [768, 1024], P('lat', 'lon'), may hold values from 3.7 to 5.5
- couplings: float32 [4, 768, 1024], P(None, 'lat', 'lon'), may hold values from 0.15 to 0.45
- land_sea: int32 [768, 1024], P('lat', 'lon'), may hold values 0 or 1
- fold_partner: int32 [1024], replicated, may hold values from 0 to 1023, as said below
Outputs:
- solution: float32 [8, 768, 1024], P(None, 'lat', 'lon')
- residual: float32 [8, 768, 1024], P(None, 'lat', 'lon')
Inputs may be any that keep to these rules, and one draw needn't show every extreme that they name: fold_partner[i] = (s - i) mod 1024 for one integer s, so fold_partner[fold_partner[i]] = i.
All inputs are finite; a program needn't handle non-finite values. No bound on the sum of `land_sea` on one device may be relied on, other than what follows from the above.
Results may differ from a plain program's by a relative error of at most 0.0003.
Values sent between devices are 32-bit elements; how exact they have to be, the bound alone decides.
A program may use at most 64 MiB of HBM per device.

v0:
```python
import functools

import jax
import jax.numpy as jnp
from jax import lax
from jax.experimental import pallas as pl
from jax.experimental.pallas import tpu as pltpu
from jax.sharding import PartitionSpec as P

ITERS = 3
MESH = pl.DeviceIdType.MESH
S_, SE_, SW_, N_, NE_, NW_ = range(6)


def kernel(
    lat_count, lon_count,
    rhs, center_hbm, coup_hbm, land_hbm, partner_hbm, w, mix,
    center, coup, land, partner,
    dmask, coef, rowtop, rowbot, colw, cole, rrow, rcol, rfold, red, rred_lon, rred_lat,
    load_sem, row_ss, row_rs, col_ss, col_rs, fold_ss, fold_rs,
    rl_ss, rl_rs, rt_ss, rt_rs,
):
    f32 = jnp.float32
    members, rows, cols = rhs.shape
    groups = rows // 8
    halves = -(-rows // 120)
    half = rows // halves
    step_rows = 24 if half % 24 == 0 else 8
    steps = half // step_rows
    la, lo = lax.axis_index("lat"), lax.axis_index("lon")
    lat_first, lat_last = la == 0, la == lat_count - 1
    north, south = lax.rem(la + 1, lat_count), lax.rem(la + lat_count - 1, lat_count)
    east, west = lax.rem(lo + 1, lon_count), lax.rem(lo + lon_count - 1, lon_count)
    lane = lax.broadcasted_iota(jnp.int32, (members, cols), 1)
    sub = lax.broadcasted_iota(jnp.int32, (8, cols), 0)

    loads = [
        pltpu.make_async_copy(center_hbm, center, load_sem.at[0]),
        pltpu.make_async_copy(coup_hbm, coup, load_sem.at[1]),
        pltpu.make_async_copy(land_hbm, land, load_sem.at[2]),
        pltpu.make_async_copy(partner_hbm, partner, load_sem.at[3]),
    ]
    for m in range(members):
        loads.append(pltpu.make_async_copy(
            rhs.at[m], w.at[0, pl.ds(0, rows), m], load_sem.at[4 + m]))
    for c in loads:
        c.start()

    barrier = pltpu.get_barrier_semaphore()
    partners = [(la, lax.rem(lo + d, lon_count)) for d in range(1, lon_count)]
    partners += [(lax.rem(la + d, lat_count), lo) for d in range(1, lat_count)]
    partners += [(north, east), (north, west), (south, east), (south, west)]
    for p in partners:
        pl.semaphore_signal(barrier, inc=1, device_id=p, device_id_type=MESH)

    for c in loads:
        c.wait()

    def roll(x, shift, axis=1):
        return pltpu.roll(x, shift, axis)

    def packed_step(pw, pe, values):
        pw, pe = roll(pw, cols - step_rows), roll(pe, cols - step_rows)
        for r, v in enumerate(values):
            at = cols - step_rows + r
            pw = jnp.where(lane == at, roll(v, at), pw)
            pe = jnp.where(lane == at, roll(v, (at + 1) % cols), pe)
        return pw, pe

    for h in range(halves):
        def prep(gl, carry):
            pw, pe = carry
            j0 = pl.multiple_of((h * steps + gl) * step_rows, 8)
            rs = pl.ds(j0, step_rows)
            dmask[rs, :] = land[rs, :].astype(f32) / center[rs, :]
            values = []
            for r in range(step_rows):
                v = w[0, j0 + r] * dmask[pl.ds(j0 + r, 1), :]
                w[0, j0 + r] = v
                values.append(v)
            return packed_step(pw, pe, values)
        zero = jnp.zeros((members, cols), f32)
        pw, pe = lax.fori_loop(0, steps, prep, (zero, zero))
        colw[0, h] = roll(pw, half)
        cole[0, h] = roll(pe, half)
    cw = jnp.zeros((8, cols), f32)
    ce = jnp.zeros((8, cols), f32)
    for g in range(groups):
        rs = pl.ds(g * 8, 8)
        ce = jnp.where(lane == g, roll(coup[0, rs, :], g + 1), ce)
        ce = jnp.where(lane == groups + g, roll(coup[2, rs, :], groups + g + 1), ce)
        cw = jnp.where(lane == g, roll(coup[3, rs, :], g) if g else coup[3, rs, :], cw)
    colw[0, halves] = cw
    cole[0, halves] = ce
    rowtop[0, 0] = w[0, rows - 1]
    rowbot[0, 0] = w[0, 0]
    top = [coup[c, pl.ds(rows - 1, 1), :] for c in range(4)]
    packed = jnp.zeros((8, cols), f32)
    for c in (1, 2, 3):
        packed = jnp.where(sub == c, top[c], packed)
    rowtop[0, 1] = packed

    pl.semaphore_wait(barrier, len(partners))

    def exchange(k, between):
        tops = 2 if k == 0 else 1
        depth = halves + 1 if k == 0 else halves
        cps = []

        def rcopy(src, slot, n, dev):
            cps.append(pltpu.make_async_remote_copy(
                src_ref=src.at[k, pl.ds(0, n)], dst_ref=rrow.at[k, slot, pl.ds(0, n)],
                send_sem=row_ss.at[k, slot], recv_sem=row_rs.at[k, slot],
                device_id=dev, device_id_type=MESH))
        rcopy(rowtop, SW_, tops, (north, east))
        rcopy(rowtop, SE_, tops, (north, west))
        rcopy(rowbot, NW_, 1, (south, east))
        rcopy(rowbot, NE_, 1, (south, west))
        rcopy(rowtop, S_, tops, (north, lo))
        rcopy(rowbot, N_, 1, (south, lo))
        for src, side, dev in ((colw, 0, west), (cole, 1, east)):
            cps.append(pltpu.make_async_remote_copy(
                src_ref=src.at[k, pl.ds(0, depth)], dst_ref=rcol.at[k, side, pl.ds(0, depth)],
                send_sem=col_ss.at[k, side], recv_sem=col_rs.at[k, side],
                device_id=(la, dev), device_id_type=MESH))
        folds = []
        for d in range(1, lon_count):
            folds.append(pltpu.make_async_remote_copy(
                src_ref=rowtop.at[k, pl.ds(0, tops)], dst_ref=rfold.at[k, d, pl.ds(0, tops)],
                send_sem=fold_ss.at[k, d], recv_sem=fold_rs.at[k, d],
                device_id=(la, lax.rem(lo + d, lon_count)), device_id_type=MESH))

        @pl.when(lat_last)
        def _():
            for c in folds:
                c.start()
        for c in cps:
            c.start()
        between()
        for c in cps:
            c.wait_recv()

        @pl.when(lat_last)
        def _():
            for c in folds:
                c.wait_recv()
        return cps, folds

    def folded(k, slot, own):
        mine = partner[pl.ds(lo, 1), :]
        out = jnp.zeros((8, cols), f32)
        for d in range(lon_count):
            data = own if d == 0 else rfold[k, d, slot]
            first = lax.rem(lo + lon_count - d, lon_count) * cols
            at = jnp.broadcast_to(mine - first, (8, cols))
            inside = jnp.logical_and(at >= 0, at < cols)
            at = jnp.clip(at, 0, cols - 1)
            got = jnp.take_along_axis(data, at, axis=1, mode="promise_in_bounds")
            out = jnp.where(inside, got, out)
        return out

    done = []
    lane8 = lax.broadcasted_iota(jnp.int32, (8, cols), 1)

    def coefficients():
        smsg, semsg, swmsg = rrow[0, S_, 1], rrow[0, SE_, 1], rrow[0, SW_, 1]
        keep = jnp.where(lat_first, 0.0, 1.0).astype(f32)
        under_n = roll(smsg, 7, 0) * keep
        under_ne = roll(roll(jnp.where(lane8 == cols - 1, swmsg, smsg), 1), 6, 0) * keep
        under_nw = roll(roll(jnp.where(lane8 == 0, semsg, smsg), cols - 1), 5, 0) * keep
        from_east, from_west = rcol[0, 0, halves], rcol[0, 1, halves]

        @pl.when(lat_last)
        def _():
            got = folded(0, 1, rowtop[0, 1])
            last = rows - 1
            coup[1, pl.ds(last, 1), :] = 0.5 * (coup[1, pl.ds(last, 1), :] + got[1:2, :])
            coup[2, pl.ds(last, 1), :] = jnp.zeros((1, cols), f32)
            coup[3, pl.ds(last, 1), :] = jnp.zeros((1, cols), f32)

        def step(g, carry):
            pn, pne, pnw = carry
            rs = pl.ds(pl.multiple_of(g * 8, 8), 8)
            d = dmask[rs, :]
            e, n, ne, nw = (coup[c, rs, :] for c in range(4))
            gw = roll(from_west, lax.rem(2 * cols - 1 - g, cols))
            gne = roll(from_west, lax.rem(2 * cols - 1 - groups - g, cols))
            gnw = roll(from_east, lax.rem(cols - g, cols))
            coef[0, rs, :] = e * d
            coef[1, rs, :] = roll(jnp.where(lane8 == cols - 1, gw, e), 1) * d
            coef[2, rs, :] = n * d
            ns = roll(n, 1, 0)
            coef[3, rs, :] = jnp.where(sub == 0, pn, ns) * d
            coef[4, rs, :] = ne * d
            nes = roll(roll(jnp.where(lane8 == cols - 1, gne, ne), 1), 1, 0)
            coef[5, rs, :] = jnp.where(sub == 0, pne, nes) * d
            coef[6, rs, :] = nw * d
            nws = roll(roll(jnp.where(lane8 == 0, gnw, nw), cols - 1), 1, 0)
            coef[7, rs, :] = jnp.where(sub == 0, pnw, nws) * d
            return ns, nes, nws
        lax.fori_loop(0, groups, step, (under_n, under_ne, under_nw), unroll=12)

    zero = jnp.zeros((members, cols), f32)
    sums = []

    def add_sums():
        for acc in accs:
            sums.append(jnp.sum(acc, axis=1, keepdims=True))

    accs = []
    for k in range(ITERS):
        done.append(exchange(k, add_sums))
        if k == 0:
            coefficients()
        w[k, rows] = rrow[k, N_, 0]

        @pl.when(lat_last)
        def _():
            w[k, rows] = folded(k, 0, w[k, rows - 1])

        def sides(v, ge, gw):
            ve = roll(jnp.where(lane == 0, ge, v), cols - 1)
            vw = roll(jnp.where(lane == cols - 1, gw, v), 1)
            return v, ve, vw

        prev = sides(rrow[k, S_, 0], rrow[k, SE_, 0], rrow[k, SW_, 0])
        gws, ges = [], []
        for h in range(halves):
            if h + 1 < halves:
                fe = roll(rcol[k, 0, h + 1], half)
                fw = roll(rcol[k, 1, h + 1], half)
            else:
                fe = roll(rrow[k, NE_, 0], half)
                fw = roll(rrow[k, NW_, 0], half + 1)
            ges.append(jnp.where(lane == half, fe, rcol[k, 0, h]))
            gws.append(jnp.where(lane == half, fw, rcol[k, 1, h]))
        cur = sides(w[k, 0], ges[0], roll(gws[0], cols - 1))
        acc0, acc1 = zero, zero
        for h in range(halves):
            ge_h, gw_h = ges[h], gws[h]

            def step(gl, carry):
                prev, cur, acc0, acc1, pw, pe, ge, gw = carry
                j0 = pl.multiple_of((h * steps + gl) * step_rows, 8)
                values = []
                for r in range(step_rows):
                    j = j0 + r
                    nxt = sides(w[k, j + 1], roll(ge, cols - 1 - r), roll(gw, cols - 2 - r))
                    c = [coef[q, pl.ds(j, 1), :] for q in range(8)]
                    out = (c[0] * cur[1] + c[1] * cur[2]) + (c[2] * nxt[0] + c[3] * prev[0])
                    out = out + ((c[4] * nxt[1] + c[5] * prev[2]) + (c[6] * nxt[2] + c[7] * prev[1]))
                    w[k + 1, j] = out
                    t = center[pl.ds(j, 1), :] * cur[0]
                    acc0 = acc0 + t * cur[0]
                    acc1 = acc1 + t * out
                    values.append(out)
                    prev, cur = cur, nxt
                if k + 1 < ITERS:
                    pw, pe = packed_step(pw, pe, values)
                ge, gw = roll(ge, cols - step_rows), roll(gw, cols - step_rows)
                return prev, cur, acc0, acc1, pw, pe, ge, gw
            prev, cur, acc0, acc1, pw, pe, _, _ = lax.fori_loop(
                0, steps, step, (prev, cur, acc0, acc1, zero, zero, ge_h, gw_h))
            if k + 1 < ITERS:
                colw[k + 1, h] = roll(pw, half)
                cole[k + 1, h] = roll(pe, half)
        if k + 1 < ITERS:
            rowtop[k + 1, 0] = w[k + 1, rows - 1]
            rowbot[k + 1, 0] = w[k + 1, 0]
        accs[:] = [acc0, acc1]
    add_sums()
    moments = zero
    for i, total in enumerate(sums):
        moments = jnp.where(lane == i, total, moments)

    def reduce(slot, value, recv, ss, rs, count, dev):
        red[slot] = value
        cps = [
            pltpu.make_async_remote_copy(
                src_ref=red.at[slot], dst_ref=recv.at[d], send_sem=ss.at[d],
                recv_sem=rs.at[d], device_id=dev(d), device_id_type=MESH)
            for d in range(1, count)
        ]
        for c in cps:
            c.start()
        for c in cps:
            c.wait_recv()
        for d in range(1, count):
            value = value + recv[d]
        return value, cps

    moments, c1 = reduce(0, moments, rred_lon, rl_ss, rl_rs, lon_count,
                         lambda d: (la, lax.rem(lo + d, lon_count)))
    moments, c2 = reduce(1, moments, rred_lat, rt_ss, rt_rs, lat_count,
                         lambda d: (lax.rem(la + d, lat_count), lo))

    m0, m1, m2, m3, m4, m5 = (
        jnp.broadcast_to(moments[:, i:i + 1], (members, cols)) for i in range(6))
    a0 = m1 / m0
    h1 = m2 - a0 * m1
    a1 = (m3 - 2.0 * a0 * m2 + a0 * a0 * m1) / h1
    b1 = h1 / m0
    p1 = -(a0 + a1)
    p0 = a0 * a1 - b1
    h2 = m4 + p1 * m3 + p0 * m2
    a2 = (m5 + p1 * m4 + p0 * m3) / h2 + p1
    b2 = h2 / h1
    t2 = p1 - a2
    t1 = p0 - a2 * p1 - b2
    t0 = b2 * a0 - a2 * p0
    q3 = 1.0 / (1.0 + t2 + t1 + t0)
    q2, q1, q0 = t2 * q3, t1 * q3, t0 * q3
    s2, s1, s0 = q3, q2 + q3, q1 + q2 + q3

    for i, value in enumerate((s0, s1, s2, q0, q1, q2, q3)):
        mix[i] = value

    for cps, folds in done:
        for cp in cps:
            cp.wait_send()

        @pl.when(lat_last)
        def _():
            for cp in folds:
                cp.wait_send()
    for cp in c1 + c2:
        cp.wait_send()


def finish(w, mix, center, sol_out, res_out, obuf, store_sem):
    members, rows, cols = sol_out.shape
    s0, s1, s2, q0, q1, q2, q3 = (mix[i] for i in range(7))
    chunk = 4
    size = rows // 8 // chunk
    stores = []
    for c in range(chunk):

        def final(g, carry):
            for r in range(8):
                j = (c * size + g) * 8 + r
                v0, v1, v2, v3 = (w[i, j] for i in range(4))
                obuf[0, j] = s0 * v0 + s1 * v1 + s2 * v2
                obuf[1, j] = center[pl.ds(j, 1), :] * (q0 * v0 + q1 * v1 + q2 * v2 + q3 * v3)
            return carry
        lax.fori_loop(0, size, final, 0)
        rs = pl.ds(c * size * 8, size * 8)
        for o, dst in ((0, sol_out), (1, res_out)):
            for m in range(members):
                cp = pltpu.make_async_copy(
                    obuf.at[o, rs, m], dst.at[m, rs], store_sem.at[c, o, m])
                cp.start()
                stores.append(cp)
    for cp in stores:
        cp.wait()


def body(lat_count, lon_count, right_side, center, couplings, land_sea, fold_partner):
    members, rows, cols = right_side.shape
    f32 = jnp.float32
    halves = -(-rows // 120)
    hbm = pl.BlockSpec(memory_space=pl.ANY)
    dma = pltpu.SemaphoreType.DMA
    shape = jax.ShapeDtypeStruct(right_side.shape, f32)
    vmem = pl.BlockSpec(memory_space=pltpu.VMEM)
    w, mix = pl.pallas_call(
        functools.partial(kernel, lat_count, lon_count),
        out_shape=(pltpu.VMEM((ITERS + 1, rows + 1, members, cols), f32),
                   pltpu.VMEM((7, members, cols), f32)),
        in_specs=[hbm] * 5,
        out_specs=(vmem, vmem),
        scratch_shapes=[
            pltpu.VMEM((rows, cols), f32),
            pltpu.VMEM((4, rows, cols), f32),
            pltpu.VMEM((rows, cols), jnp.int32),
            pltpu.VMEM((lon_count, cols), jnp.int32),
            pltpu.VMEM((rows, cols), f32),
            pltpu.VMEM((8, rows, cols), f32),
            pltpu.VMEM((ITERS, 2, 8, cols), f32),
            pltpu.VMEM((ITERS, 1, 8, cols), f32),
            pltpu.VMEM((ITERS, halves + 1, 8, cols), f32),
            pltpu.VMEM((ITERS, halves + 1, 8, cols), f32),
            pltpu.VMEM((ITERS, 6, 2, 8, cols), f32),
            pltpu.VMEM((ITERS, 2, halves + 1, 8, cols), f32),
            pltpu.VMEM((ITERS, lon_count, 2, 8, cols), f32),
            pltpu.VMEM((2, 8, cols), f32),
            pltpu.VMEM((lon_count, 8, cols), f32),
            pltpu.VMEM((lat_count, 8, cols), f32),
            dma((4 + members,)),
            dma((ITERS, 6)), dma((ITERS, 6)),
            dma((ITERS, 2)), dma((ITERS, 2)),
            dma((ITERS, lon_count)), dma((ITERS, lon_count)),
            dma((lon_count,)), dma((lon_count,)),
            dma((lat_count,)), dma((lat_count,)),
        ],
        compiler_params=pltpu.CompilerParams(
            collective_id=0, has_side_effects=True, vmem_limit_bytes=32 * 1024 * 1024),
    )(right_side, center, couplings, land_sea, fold_partner.reshape(lon_count, cols))
    return pl.pallas_call(
        finish,
        out_shape=(shape, shape),
        in_specs=[vmem] * 3,
        out_specs=(hbm, hbm),
        scratch_shapes=[
            pltpu.VMEM((2, rows, members, cols), f32),
            dma((4, 2, members)),
        ],
        compiler_params=pltpu.CompilerParams(vmem_limit_bytes=32 * 1024 * 1024),
    )(w, mix, center)


def solution(mesh):
    return jax.shard_map(
        functools.partial(body, mesh.shape["lat"], mesh.shape["lon"]),
        mesh=mesh,
        in_specs=(
            P(None, "lat", "lon"),
            P("lat", "lon"),
            P(None, "lat", "lon"),
            P("lat", "lon"),
            P(),
        ),
        out_specs=(P(None, "lat", "lon"), P(None, "lat", "lon")),
        check_vma=False,
    )
```

profile of v0, /device:TPU:0, one launch (start us, length us, event | category | flops | bytes accessed | tf_op | source)
XLA Modules:
  0.0 42.1 jit_solution(11511509566013277601)
XLA Ops:
  0.6 0.0 copy-start
  0.6 1.1 %copy-done = f32[8,192,128]{2,1,0:T(8,128)S(1)} copy-done((f32[8,192,128]{2,1,0:T(8,128)S(1)}, f32[8,192,128]{2,1,0:T(8,128)}, u32[]{:S(2)}) %copy-start) | copy-done | bytes 786456
  1.8 0.0 copy-start.1
  1.8 0.9 %copy-done.1 = f32[192,128]{1,0:T(8,128)S(1)} copy-done((f32[192,128]{1,0:T(8,128)S(1)}, f32[192,128]{1,0:T(8,128)}, u32[]{:S(2)}) %copy-start.1) | copy-done | bytes 98328
  2.7 0.0 copy-start.2
  2.7 1.0 %copy-done.2 = f32[4,192,128]{2,1,0:T(8,128)S(1)} copy-done((f32[4,192,128]{2,1,0:T(8,128)S(1)}, f32[4,192,128]{2,1,0:T(8,128)}, u32[]{:S(2)}) %copy-start.2) | copy-done | bytes 393240
  3.7 0.0 copy-start.3
  3.7 0.9 %copy-done.3 = s32[192,128]{1,0:T(8,128)S(1)} copy-done((s32[192,128]{1,0:T(8,128)S(1)}, s32[192,128]{1,0:T(8,128)}, u32[]{:S(2)}) %copy-start.3) | copy-done | bytes 98328
  4.5 0.0 copy-start.4
  4.5 0.7 %copy-done.4 = s32[1024]{0:T(1024)S(1)} copy-done((s32[1024]{0:T(1024)S(1)}, s32[1024]{0:T(1024)}, u32[]{:S(2)}) %copy-start.4) | copy-done | bytes 4120
  5.2 35.1 %shard_map.68 = (f32[4,193,8,128]{3,2,1,0:T(8,128)S(1)}, f32[7,8,128]{2,1,0:T(8,128)S(1)}) custom-call(f32[8,192,128]{2,1,0:T(8,128)S(1)} %copy-done, f32[192,128]{1,0:T(8,128)S(1)} %copy-done.1, f32[4,192,128]{2,1,0:T(8,128)S(1)} %copy-done.2, s32[192,128]{1,0:T(8,128)S(1)} %copy-done.3, s32[8,128]{1,0:T(8,128)S(1)} %bitcast.1), custom_call_target="tpu_custom_call" | custom-call | tf_op jit(solution)/shard_map/pallas_call | solution.py:365
  40.3 1.8 %shard_map.69 = (f32[8,192,128]{2,1,0:T(8,128)}, f32[8,192,128]{2,1,0:T(8,128)}) custom-call(f32[4,193,8,128]{3,2,1,0:T(8,128)S(1)} %get-tuple-element.4.w, f32[7,8,128]{2,1,0:T(8,128)S(1)} %get-tuple-element.5.mix, f32[192,128]{1,0:T(8,128)S(1)} %copy-done.1), custom_call_target="tpu_custom_call" | custom-call | tf_op jit(solution)/shard_map/pallas_call | solution.py:398
Async XLA Ops:
  0.6 1.1 %copy-start = (f32[8,192,128]{2,1,0:T(8,128)S(1)}, f32[8,192,128]{2,1,0:T(8,128)}, u32[]{:S(2)}) copy-start(f32[8,192,128]{2,1,0:T(8,128)} %rhs.1) | copy-start | bytes 2359300
  1.8 0.9 %copy-start.1 = (f32[192,128]{1,0:T(8,128)S(1)}, f32[192,128]{1,0:T(8,128)}, u32[]{:S(2)}) copy-start(f32[192,128]{1,0:T(8,128)} %center.1) | copy-start | bytes 294916
  2.7 1.0 %copy-start.2 = (f32[4,192,128]{2,1,0:T(8,128)S(1)}, f32[4,192,128]{2,1,0:T(8,128)}, u32[]{:S(2)}) copy-start(f32[4,192,128]{2,1,0:T(8,128)} %coup_hbm.1) | copy-start | bytes 1179652
  3.7 0.9 %copy-start.3 = (s32[192,128]{1,0:T(8,128)S(1)}, s32[192,128]{1,0:T(8,128)}, u32[]{:S(2)}) copy-start(s32[192,128]{1,0:T(8,128)} %land_hbm.1) | copy-start | bytes 294916
  4.5 0.7 %copy-start.4 = (s32[1024]{0:T(1024)S(1)}, s32[1024]{0:T(1024)}, u32[]{:S(2)}) copy-start(s32[1024]{0:T(1024)} %param.9) | copy-start | bytes 12292
where the time goes:
time: 42.4 us; the launch traced here: 42.1 us
  Pallas kernels  36.9 us (87%)
  local copies, waits for them, and re-layouts  4.59 us (11%)
  between operations  0.65 us (2%)
    pallas_call x1, Pallas kernels, body(): pl.pallas_call(functools.partial(kernel, lat_count, lon_count), out_shape...  35.1 us
    unnamed x10, local copies, waits for them, and re-layouts  4.59 us
    pallas_call x1, Pallas kernels, body(): pl.pallas_call(finish, out_shape=(shape, shape), in_specs=[vmem] * 3, out...  1.82 us

commit v1 on v0

v1 whole, which is shorter than its diff:
```python
import functools

import jax
import jax.numpy as jnp
from jax import lax
from jax.experimental import pallas as pl
from jax.experimental.pallas import tpu as pltpu
from jax.sharding import PartitionSpec as P

ITERS = 3
MESH = pl.DeviceIdType.MESH
EDGE = 16
SLOT = 16
STRIP, KSTRIP, EAST, NORTH, NEAST, NWEST, SCALE, ARRAYS = range(8, 16)
COUPLED = (EAST, NORTH, NEAST, NWEST, SCALE)
FROM_S, FROM_N, FROM_SW, FROM_SE, FROM_NW, FROM_NE, FROM_W, FROM_E = range(8)


def roll(x, shift, axis=1):
    return pltpu.roll(x, shift, axis)


def kernel(
    lat_count, lon_count,
    rhs, center_hbm, coup_hbm, land_hbm, partner_hbm, st, vk, mix, cen,
    land, partner, strips, coefm, coefs, pack, packin, rowin, diagin, fold,
    macc, red, redlon, redlat,
    load_sem, send_sem, recv_sem, fold_ss, fold_rs, lon_ss, lon_rs, lat_ss, lat_rs,
):
    f32 = jnp.float32
    members, rows, cols = rhs.shape
    tiles = rows // 8
    first, last = 2, tiles + 1
    inner = tiles - 2
    unroll = max(u for u in range(1, 12) if inner % u == 0)
    la, lo = lax.axis_index("lat"), lax.axis_index("lon")
    lat_first, lat_last = la == 0, la == lat_count - 1
    not_first, not_last = la > 0, la < lat_count - 1
    north, south = lax.rem(la + 1, lat_count), lax.rem(la + lat_count - 1, lat_count)
    east, west = lax.rem(lo + 1, lon_count), lax.rem(lo + lon_count - 1, lon_count)
    lane = lax.broadcasted_iota(jnp.int32, (8, cols), 1)
    sub = lax.broadcasted_iota(jnp.int32, (8, cols), 0)
    place = jnp.bitwise_and(lane, SLOT - 1)
    group = lax.shift_right_logical(lane, 4)
    zero = jnp.zeros((8, cols), f32)

    def at(tile):
        start = tile * 8
        return pl.ds(start if isinstance(start, int) else pl.multiple_of(start, 8), 8)

    own = pl.ds(EDGE, rows)
    loads = [
        pltpu.make_async_copy(center_hbm, cen, load_sem.at[0]),
        pltpu.make_async_copy(land_hbm, land, load_sem.at[1]),
        pltpu.make_async_copy(partner_hbm.at[pl.ds(0, 1)], partner, load_sem.at[2]),
        pltpu.make_async_copy(coup_hbm, st.at[pl.ds(EAST, 4), own], load_sem.at[3]),
        pltpu.make_async_copy(rhs, st.at[pl.ds(0, members), own], load_sem.at[4]),
    ]
    for c in loads:
        c.start()

    barrier = pltpu.get_barrier_semaphore()
    partners = [(la, lax.rem(lo + d, lon_count)) for d in range(1, lon_count)]
    partners += [(lax.rem(la + d, lat_count), lo) for d in range(1, lat_count)]
    partners += [(north, east), (north, west), (south, east), (south, west)]
    for p in partners:
        pl.semaphore_signal(barrier, inc=1, device_id=p, device_id_type=MESH)

    for c in loads:
        c.wait()

    inside_w = jnp.logical_and(place >= 3, place < 8)
    inside_e = jnp.logical_and(place >= 8, place < 13)

    def own_strip(arrays):
        out = zero
        for g, x in enumerate(arrays):
            mine = group == g
            out = jnp.where(jnp.logical_and(mine, inside_w), roll(x, g * SLOT + 3), out)
            out = jnp.where(jnp.logical_and(mine, inside_e),
                            roll(x, (g * SLOT + 13) % cols), out)
        return out

    def prep(t, carry):
        pe, pw, ke, kw = zero, zero, zero, zero
        for q in range(4):
            tile = first + t * 4 + q
            rs = at(tile)
            near = at(tile - first)
            d = land[near, :].astype(f32) / cen[near, :]
            st[SCALE, rs, :] = d
            vals = []
            for m in range(members):
                v = st[m, rs, :] * d
                st[m, rs, :] = v
                vals.append(v)
            s = own_strip(vals)
            st[STRIP, rs, :] = s
            k = own_strip([st[c, rs, :] for c in COUPLED[:4]] + [d])
            st[KSTRIP, rs, :] = k
            mine = lax.shift_right_logical(place, 2) == q
            pe = jnp.where(mine, roll(s, (4 * q - 10) % cols), pe)
            pw = jnp.where(mine, roll(s, (4 * q - 3) % cols), pw)
            ke = jnp.where(mine, roll(k, (4 * q - 10) % cols), ke)
            kw = jnp.where(mine, roll(k, (4 * q - 3) % cols), kw)
        pack[0, 0, t] = pe
        pack[0, 1, t] = ke
        pack[1, 0, t] = pw
        pack[1, 1, t] = kw
        return carry
    lax.fori_loop(0, tiles // 4, prep, 0)

    top, bottom = pl.ds(EDGE + rows - 3, 3), pl.ds(EDGE, 3)

    def remote(src, dst, slot, dev):
        return pltpu.make_async_remote_copy(
            src_ref=src, dst_ref=dst, send_sem=send_sem.at[slot], recv_sem=recv_sem.at[slot],
            device_id=dev, device_id_type=MESH)

    sides = [remote(pack.at[0], packin.at[0], FROM_W, (la, east)),
             remote(pack.at[1], packin.at[1], FROM_E, (la, west))]
    pair = pl.ds(STRIP, 2)
    low, high = pl.ds(5, 3), pl.ds(0, 3)
    up = [remote(st.at[:, top], rowin.at[0, :, low], FROM_S, (north, lo)),
          remote(st.at[pair, top], diagin.at[0, :, low], FROM_SW, (north, east)),
          remote(st.at[pair, top], diagin.at[1, :, low], FROM_SE, (north, west))]
    down = [remote(st.at[:, bottom], rowin.at[1, :, high], FROM_N, (south, lo)),
            remote(st.at[pair, bottom], diagin.at[2, :, high], FROM_NW, (south, east)),
            remote(st.at[pair, bottom], diagin.at[3, :, high], FROM_NE, (south, west))]
    folds = [
        pltpu.make_async_remote_copy(
            src_ref=fold.at[0, :, high], dst_ref=fold.at[d, :, high],
            send_sem=fold_ss.at[d], recv_sem=fold_rs.at[d],
            device_id=(la, lax.rem(lo + d, lon_count)), device_id_type=MESH)
        for d in range(1, lon_count)
    ]
    fold_arrays = list(range(members)) + list(COUPLED)

    pl.semaphore_wait(barrier, len(partners))
    for c in sides:
        c.start()

    @pl.when(lat_last)
    def _():
        end = EDGE + rows - 1
        for i, a in enumerate(fold_arrays):
            if a == NORTH:
                picks = (end - 1, end - 2, end)
            elif a in (NEAST, NWEST):
                picks = (end - 1, end - 2, end - 2)
            else:
                picks = (end, end - 1, end - 2)
            for g, r in enumerate(picks):
                fold[0, i, pl.ds(g, 1), :] = st[a, pl.ds(r, 1), :]
        for c in folds:
            c.start()

    @pl.when(not_last)
    def _():
        for c in up:
            c.start()

    @pl.when(not_first)
    def _():
        for c in down:
            c.start()

    for c in sides:
        c.wait_recv()

    def merge(t, carry):
        for g in range(2):
            fw, fe = packin[0, g, t], packin[1, g, t]
            for q in range(4):
                rs = at(first + t * 4 + q)
                x = st[STRIP + g, rs, :]
                x = jnp.where(place < 3, roll(fw, (-4 * q) % cols) if q else fw, x)
                x = jnp.where(place > 12, roll(fe, 13 - 4 * q), x)
                strips[0, g, rs, :] = x
        return carry
    lax.fori_loop(0, tiles // 4, merge, 0)

    def lateral(x, s, g):
        xe = jnp.where(lane == cols - 1, roll(s, lax.rem(2 * cols - 14 - SLOT * g, cols)),
                       roll(x, cols - 1))
        xw = jnp.where(lane == 0, roll(s, lax.rem(2 * cols - 2 - SLOT * g, cols)), roll(x, 1))
        return xe, xw

    def main_coefs(tile):
        rs = at(tile)
        start = tile * 8
        below = pl.ds(start - 1, 8)
        above = pl.ds(start + 1, 8)
        k = strips[0, 1, rs, :]

        def from_west(a, g):
            return jnp.where(lane == 0, roll(k, cols - 2 - SLOT * g), roll(st[a, rs, :], 1))
        d, dn = st[SCALE, rs, :], st[SCALE, above, :]
        ds_ = st[SCALE, below, :]
        coefm[0, rs, :] = d * st[EAST, rs, :]
        coefm[1, rs, :] = d * from_west(EAST, 0)
        coefm[2, rs, :] = ds_ * st[NORTH, below, :]
        coefm[3, rs, :] = ds_ * st[NEAST, below, :]
        coefm[4, rs, :] = ds_ * st[NWEST, below, :]
        coefm[5, rs, :] = dn * st[NORTH, rs, :]
        coefm[6, rs, :] = dn * jnp.where(lane == cols - 1, roll(k, cols - 14 - SLOT * 3),
                                         roll(st[NWEST, rs, :], cols - 1))
        coefm[7, rs, :] = dn * from_west(NEAST, 2)

    def strip_coefs(tile):
        rs = at(tile)
        start = tile * 8
        here = strips[0, 1, rs, :]
        below = strips[0, 1, pl.ds(start - 1, 8), :]
        above = strips[0, 1, pl.ds(start + 1, 8), :]

        def spread(x, g, shift=0):
            where = jnp.bitwise_and(place + (g * SLOT + shift), cols - 1)
            return jnp.take_along_axis(x, where, axis=1, mode="promise_in_bounds")
        d, ds_, dn = spread(here, 4), spread(below, 4), spread(above, 4)
        coefs[0, rs, :] = d * spread(here, 0)
        coefs[1, rs, :] = d * spread(here, 0, -1)
        coefs[2, rs, :] = ds_ * spread(below, 1)
        coefs[3, rs, :] = ds_ * spread(below, 2)
        coefs[4, rs, :] = ds_ * spread(below, 3)
        coefs[5, rs, :] = dn * spread(here, 1)
        coefs[6, rs, :] = dn * spread(here, 3, 1)
        coefs[7, rs, :] = dn * spread(here, 2, -1)

    def all_coefs(t, carry):
        main_coefs(first + t)
        strip_coefs(first + t)
        return carry
    lax.fori_loop(0, tiles, all_coefs, 0, unroll=4)

    def parts(x, xe, xw, c):
        cross = c[0] * xe + c[1] * xw
        upper = c[2] * x + (c[3] * xe + c[4] * xw)
        lower = c[5] * x + (c[6] * xe + c[7] * xw)
        return cross, upper, lower

    def shift_up(u, u_next):
        return roll(jnp.where(sub == 0, u_next, u), 7, 0)

    def shift_down(d_prev, d):
        return roll(jnp.where(sub == 7, d_prev, d), 1, 0)

    def source(k, g, rs):
        return st[g, rs, :] if k == 0 else vk[k - 1, g, rs, :]

    def strip_parts(k, tile):
        rs = at(tile)
        x = strips[k, 0, rs, :]
        return parts(x, roll(x, cols - 1), roll(x, 1), [coefs[q, rs, :] for q in range(8)])

    def member_parts(k, g, tile, c=None):
        rs = at(tile)
        x = source(k, g, rs)
        xe, xw = lateral(x, strips[k, 0, rs, :], g)
        if c is None:
            c = [coefm[q, rs, :] for q in range(8)]
        return x, parts(x, xe, xw, c)

    for k in range(ITERS - 1):
        cross, upper, lower = strip_parts(k, first)

        def strip_step(b, carry):
            sofar, u_old, d_old = carry
            for u in range(unroll):
                tile = first + 1 + b * unroll + u
                cross, upper, lower = strip_parts(k, tile)
                strips[k + 1, 0, at(tile - 1), :] = sofar + shift_up(u_old, upper)
                sofar, u_old, d_old = cross + shift_down(d_old, lower), upper, lower
            return sofar, u_old, d_old
        sofar, u_old, d_old = lax.fori_loop(
            0, inner // unroll, strip_step, (cross + shift_down(zero, lower), upper, lower))
        cross, upper, lower = strip_parts(k, last)
        strips[k + 1, 0, at(last - 1), :] = sofar + shift_up(u_old, upper)
        strips[k + 1, 0, at(last), :] = cross + shift_down(d_old, lower) + shift_up(upper, zero)

    batch = 2
    for k in range(ITERS):
        def sweep(p, carry):
            gs = [p * batch + i for i in range(batch)]
            state = []
            for g in gs:
                _, (cross, upper, lower) = member_parts(k, g, first)
                state.append((cross + shift_down(zero, lower), upper, lower, zero, zero, zero))

            def step(b, state):
                state = list(state)
                for u in range(unroll):
                    tile = first + 1 + b * unroll + u
                    rs = at(tile)
                    c = [coefm[q, rs, :] for q in range(8)]
                    weight = cen[at(tile - first), :]
                    for i, g in enumerate(gs):
                        sofar, u_old, d_old, w_old, acc0, acc1 = state[i]
                        x, (cross, upper, lower) = member_parts(k, g, tile, c)
                        out = sofar + shift_up(u_old, upper)
                        vk[k, g, at(tile - 1), :] = out
                        acc1 = acc1 + w_old * out
                        w = weight * x
                        acc0 = acc0 + w * x
                        state[i] = (cross + shift_down(d_old, lower), upper, lower, w, acc0, acc1)
                return tuple(state)
            state = lax.fori_loop(0, inner // unroll, step, tuple(state))
            for i, g in enumerate(gs):
                sofar, u_old, d_old, w_old, acc0, acc1 = state[i]
                _, (cross, upper, lower) = member_parts(k, g, last)
                out = sofar + shift_up(u_old, upper)
                vk[k, g, at(last - 1), :] = out
                vk[k, g, at(last), :] = cross + shift_down(d_old, lower) + shift_up(upper, zero)
                macc[2 * k, g] = acc0
                macc[2 * k + 1, g] = acc1 + w_old * out
            return carry
        lax.fori_loop(0, members // batch, sweep, 0)

    @pl.when(not_first)
    def _():
        for s in (FROM_S, FROM_SW, FROM_SE):
            up[s if s == FROM_S else s - FROM_SW + 1].wait_recv()
        rs = at(first - 1)
        for a in range(ARRAYS):
            if a not in (STRIP, KSTRIP):
                st[a, rs, :] = rowin[0, a]
        for g in range(2):
            x = rowin[0, STRIP + g]
            x = jnp.where(place < 3, roll(diagin[0, g], cols - 10), x)
            strips[0, g, rs, :] = jnp.where(place > 12, roll(diagin[1, g], 10), x)

    @pl.when(lat_first)
    def _():
        rs = at(first - 1)
        for a in range(ARRAYS):
            st[a, rs, :] = zero
        for g in range(2):
            strips[0, g, rs, :] = zero

    @pl.when(not_last)
    def _():
        for c in down:
            c.wait_recv()
        rs = at(last + 1)
        for a in range(ARRAYS):
            if a not in (STRIP, KSTRIP):
                st[a, rs, :] = rowin[1, a]
        for g in range(2):
            x = rowin[1, STRIP + g]
            x = jnp.where(place < 3, roll(diagin[2, g], cols - 10), x)
            strips[0, g, rs, :] = jnp.where(place > 12, roll(diagin[3, g], 10), x)

    @pl.when(lat_last)
    def _():
        for c in folds:
            c.wait_recv()
        total = lon_count * cols
        rs = at(last + 1)
        shown = jnp.where(place < 8, place - 3, place + (cols - 13))
        origin = lax.rem(partner[0, 0] - lo * cols + total, total)

        def view(shift):
            start = lax.rem(origin + shift + total, total)
            chunk = lax.div(start, cols)
            head = start - chunk * cols
            slots = [lax.rem(lo - chunk - o + 3 * lon_count, lon_count) for o in (1, 0, -1, -2)]
            z = head - shown
            return (slots, jnp.bitwise_and(head - lane, cols - 1), lane <= head,
                    jnp.bitwise_and(z, cols - 1), (z >= cols, z >= 0, z >= -cols))

        def take(x, where):
            return jnp.take_along_axis(x, where, axis=1, mode="promise_in_bounds")
        views = {s: view(s) for s in (-1, 0, 1)}
        shifts = {EAST: -1, NEAST: -1, NWEST: 1}
        ghost = [zero, zero]
        for i, a in enumerate(fold_arrays):
            slots, where, within, where_s, (far, near, back) = views[shifts.get(a, 0)]
            chunks = [fold[s, i] for s in slots]
            block = jnp.where(within, take(chunks[1], where), take(chunks[2], where))
            st[a, rs, :] = block
            x = jnp.where(back, take(chunks[2], where_s), take(chunks[3], where_s))
            x = jnp.where(near, take(chunks[1], where_s), x)
            x = jnp.where(far, take(chunks[0], where_s), x)
            s, g = (0, a) if a < members else (1, COUPLED.index(a))
            ghost[s] = jnp.where(group == g, x, ghost[s])
            if a == NORTH:
                end = pl.ds(EDGE + rows - 1, 1)
                st[NORTH, end, :] = 0.5 * (st[NORTH, end, :] + block[2:3, :])
                mixed = 0.5 * (strips[0, 1, end, :] + x[2:3, :])
                g1 = group[0:1, :]
                dropped = jnp.logical_or(g1 == 2, g1 == 3)
                strips[0, 1, end, :] = jnp.where(
                    dropped, 0.0, jnp.where(g1 == 1, mixed, strips[0, 1, end, :]))
                st[NEAST, end, :] = jnp.zeros((1, cols), f32)
                st[NWEST, end, :] = jnp.zeros((1, cols), f32)
        for s in range(2):
            strips[0, s, rs, :] = ghost[s]

    for tile in (first - 1, first, last, last + 1):
        main_coefs(tile)
        strip_coefs(tile)

    def join(lo_parts, mid, hi_parts):
        out = mid[0]
        out = out + shift_down(zero if lo_parts is None else lo_parts[2], mid[2])
        return out + shift_up(mid[1], zero if hi_parts is None else hi_parts[1])

    for k in range(ITERS - 1):
        b = [strip_parts(k, t) for t in (first - 1, first, first + 1)]
        t = [strip_parts(k, t) for t in (last - 1, last, last + 1)]
        strips[k + 1, 0, at(first - 1), :] = join(None, b[0], b[1])
        strips[k + 1, 0, at(first), :] = join(b[0], b[1], b[2])
        strips[k + 1, 0, at(last), :] = join(t[0], t[1], t[2])
        strips[k + 1, 0, at(last + 1), :] = join(t[1], t[2], None)
    for k in range(ITERS):
        def band(p, carry):
            for i in range(batch):
                g = p * batch + i
                b = [member_parts(k, g, t) for t in (first - 1, first, first + 1)]
                t = [member_parts(k, g, t) for t in (last - 1, last, last + 1)]
                if k + 1 < ITERS:
                    vk[k, g, at(first - 1), :] = join(None, b[0][1], b[1][1])
                    vk[k, g, at(last + 1), :] = join(t[1][1], t[2][1], None)
                acc0, acc1 = macc[2 * k, g], macc[2 * k + 1, g]
                for tile, three in ((first, b), (last, t)):
                    out = join(three[0][1], three[1][1], three[2][1])
                    vk[k, g, at(tile), :] = out
                    x = three[1][0]
                    w = cen[at(tile - first), :] * x
                    acc0 = acc0 + w * x
                    acc1 = acc1 + w * out
                macc[2 * k, g] = acc0
                macc[2 * k + 1, g] = acc1
            return carry
        lax.fori_loop(0, members // batch, band, 0)

    row = zero
    for i in range(2 * ITERS):
        total = macc[i, :, 0, :]
        for s in range(1, 8):
            total = total + macc[i, :, s, :]
        total = jnp.sum(total, axis=1, keepdims=True)
        row = jnp.where(lane == 8 * i + sub, total, row)

    def column_sum(x):
        for s in (4, 2, 1):
            x = x + roll(x, s, 0)
        return x
    row = column_sum(row)

    def reduce(value, slot, recv, me, ss, rs, count, dev):
        red[slot] = value
        cps = [
            pltpu.make_async_remote_copy(
                src_ref=red.at[slot, pl.ds(0, 1)], dst_ref=recv.at[me, pl.ds(0, 1)],
                send_sem=ss.at[d], recv_sem=rs.at[d], device_id=dev(d), device_id_type=MESH)
            for d in range(1, count)
        ]
        for c in cps:
            c.start()
        recv[me] = value
        for c in cps:
            c.wait_recv()
        out = recv[0, pl.ds(0, 1), :]
        for d in range(1, count):
            out = out + recv[d, pl.ds(0, 1), :]
        return jnp.broadcast_to(out, (8, cols)), cps

    row, c1 = reduce(row, 0, redlon, lo, lon_ss, lon_rs, lon_count,
                     lambda d: (la, lax.rem(lo + d, lon_count)))
    row, c2 = reduce(row, 1, redlat, la, lat_ss, lat_rs, lat_count,
                     lambda d: (lax.rem(la + d, lat_count), lo))

    m0, m1, m2, m3, m4, m5 = (
        jnp.broadcast_to(
            jnp.sum(jnp.where(lane == 8 * i + sub, row, 0.0), axis=1, keepdims=True), (8, cols))
        for i in range(2 * ITERS))
    a0 = m1 / m0
    h1 = m2 - a0 * m1
    a1 = (m3 - 2.0 * a0 * m2 + a0 * a0 * m1) / h1
    b1 = h1 / m0
    p1 = -(a0 + a1)
    p0 = a0 * a1 - b1
    h2 = m4 + p1 * m3 + p0 * m2
    a2 = (m5 + p1 * m4 + p0 * m3) / h2 + p1
    b2 = h2 / h1
    t2 = p1 - a2
    t1 = p0 - a2 * p1 - b2
    t0 = b2 * a0 - a2 * p0
    q3 = 1.0 / (1.0 + t2 + t1 + t0)
    q2, q1, q0 = t2 * q3, t1 * q3, t0 * q3
    for i, value in enumerate((q3 + q2 + q1, q2 + q3, q3, q0, q1, q2, q3)):
        mix[i] = value

    for c in sides + c1 + c2:
        c.wait_send()

    @pl.when(not_last)
    def _():
        for c in up:
            c.wait_send()

    @pl.when(not_first)
    def _():
        for c in down:
            c.wait_send()

    @pl.when(lat_last)
    def _():
        for c in folds:
            c.wait_send()


def finish(st, vk, mix, center, sol_out, res_out, obuf, store_sem):
    members, rows, cols = sol_out.shape

    def one(m, carry):
        s0, s1, s2, q0, q1, q2, q3 = (
            jnp.broadcast_to(mix[i, pl.ds(m, 1), :], (8, cols)) for i in range(7))
        for t in range(rows // 8):
            here, rs = pl.ds(8 * t, 8), pl.ds(EDGE + 8 * t, 8)
            v0, v1, v2, v3 = st[m, rs, :], vk[0, m, rs, :], vk[1, m, rs, :], vk[2, m, rs, :]
            obuf[0, m, here, :] = s0 * v0 + s1 * v1 + s2 * v2
            obuf[1, m, here, :] = center[here, :] * (q0 * v0 + q1 * v1 + q2 * v2 + q3 * v3)
        for o, dst in ((0, sol_out), (1, res_out)):
            pltpu.make_async_copy(obuf.at[o, m], dst.at[m], store_sem.at[o, m]).start()
        return carry
    lax.fori_loop(0, members, one, 0)
    for m in range(members):
        for o, dst in ((0, sol_out), (1, res_out)):
            pltpu.make_async_copy(obuf.at[o, m], dst.at[m], store_sem.at[o, m]).wait()


def body(lat_count, lon_count, right_side, center, couplings, land_sea, fold_partner):
    members, rows, cols = right_side.shape
    f32 = jnp.float32
    hbm = pl.BlockSpec(memory_space=pltpu.HBM)
    vmem = pl.BlockSpec(memory_space=pltpu.VMEM)
    dma = pltpu.SemaphoreType.DMA
    shape = jax.ShapeDtypeStruct(right_side.shape, f32)
    high = rows + 2 * EDGE
    tiles = rows // 8
    folded = members + len(COUPLED)
    st, vk, mix, cen = pl.pallas_call(
        functools.partial(kernel, lat_count, lon_count),
        out_shape=(pltpu.VMEM((ARRAYS, high, cols), f32),
                   pltpu.VMEM((ITERS, members, high, cols), f32),
                   pltpu.VMEM((7, 8, cols), f32),
                   pltpu.VMEM((rows, cols), f32)),
        in_specs=[hbm] * 5,
        out_specs=(vmem, vmem, vmem, vmem),
        scratch_shapes=[
            pltpu.VMEM((rows, cols), jnp.int32),
            pltpu.SMEM((1, cols), jnp.int32),
            pltpu.VMEM((ITERS, 2, high, cols), f32),
            pltpu.VMEM((8, high, cols), f32),
            pltpu.VMEM((8, high, cols), f32),
            pltpu.VMEM((2, 2, tiles // 4, 8, cols), f32),
            pltpu.VMEM((2, 2, tiles // 4, 8, cols), f32),
            pltpu.VMEM((2, ARRAYS, 8, cols), f32),
            pltpu.VMEM((4, 2, 8, cols), f32),
            pltpu.VMEM((lon_count, folded, 8, cols), f32),
            pltpu.VMEM((2 * ITERS, members, 8, cols), f32),
            pltpu.VMEM((2, 8, cols), f32),
            pltpu.VMEM((lon_count, 8, cols), f32),
            pltpu.VMEM((lat_count, 8, cols), f32),
            dma((5,)), dma((8,)), dma((8,)),
            dma((lon_count,)), dma((lon_count,)),
            dma((lon_count,)), dma((lon_count,)),
            dma((lat_count,)), dma((lat_count,)),
        ],
        compiler_params=pltpu.CompilerParams(
            collective_id=0, has_side_effects=True, vmem_limit_bytes=32 * 1024 * 1024),
    )(*(pltpu.with_memory_space_constraint(x, pltpu.HBM) for x in (
        right_side, center, couplings, land_sea, fold_partner.reshape(lon_count, cols))))
    return pl.pallas_call(
        finish,
        out_shape=(shape, shape),
        in_specs=[vmem] * 4,
        out_specs=(hbm, hbm),
        scratch_shapes=[
            pltpu.VMEM((2, members, rows, cols), f32),
            dma((2, members)),
        ],
        compiler_params=pltpu.CompilerParams(vmem_limit_bytes=16 * 1024 * 1024),
    )(st, vk, mix, cen)


def solution(mesh):
    return jax.shard_map(
        functools.partial(body, mesh.shape["lat"], mesh.shape["lon"]),
        mesh=mesh,
        in_specs=(
            P(None, "lat", "lon"),
            P("lat", "lon"),
            P(None, "lat", "lon"),
            P("lat", "lon"),
            P(),
        ),
        out_specs=(P(None, "lat", "lon"), P(None, "lat", "lon")),
        check_vma=False,
    )
```

time: 42.4 us -> 29.9 us (0.71)
  Pallas kernels: 36.9 us -> 29.1 us
  local copies, waits for them, and re-layouts: 4.59 us -> 0 us
    pallas_call x1, Pallas kernels: 35.1 us -> 27.8 us  [body(): pl.pallas_call(functools.partial(kernel, lat_count, lon_count), out_shape...]
    unnamed x10 -> x0, local copies, waits for them, and re-layouts: 4.59 us -> none
    pallas_call x1, Pallas kernels: 1.82 us -> 1.31 us  [body(): pl.pallas_call(finish, out_shape=(shape, shape), in_specs=[vmem] * 4, out...]
where the time goes in v1:
time: 29.9 us; the launch traced here: 29.7 us
  Pallas kernels  29.1 us (97%)
  between operations  0.64 us (2%)
    pallas_call x1, Pallas kernels, body(): pl.pallas_call(functools.partial(kernel, lat_count, lon_count), out_shape...  27.8 us
    pallas_call x1, Pallas kernels, body(): pl.pallas_call(finish, out_shape=(shape, shape), in_specs=[vmem] * 4, out...  1.31 us

profile of v1, /device:TPU:0, one launch (start us, length us, event | category | flops | bytes accessed | tf_op | source)
XLA Modules:
  0.0 29.7 jit_solution(7685755149887814761)
XLA Ops:
  0.6 27.8 %shard_map.68 = (f32[15,224,128]{2,1,0:T(8,128)S(1)}, f32[3,8,224,128]{3,2,1,0:T(8,128)S(1)}, f32[7,8,128]{2,1,0:T(8,128)S(1)}, f32[192,128]{1,0:T(8,128)S(1)}) custom-call(f32[8,192,128]{2,1,0:T(8,128)} %rhs.1, f32[192,128]{1,0:T(8,128)} %center_hbm.1, f32[4,192,128]{2,1,0:T(8,128)} %coup_hbm.1, s32[192,128]{1,0:T(8,128)} %land_hbm.1, s32[8,128]{1,0:T(8,128)} %bitcast.1), custom_call_target="tpu_custom_call" | custom-call | tf_op jit(solution)/shard_map/pallas_call | solution.py:544
  28.4 1.3 %shard_map.69 = (f32[8,192,128]{2,1,0:T(8,128)}, f32[8,192,128]{2,1,0:T(8,128)}) custom-call(f32[15,224,128]{2,1,0:T(8,128)S(1)} %get-tuple-element.6.st, f32[3,8,224,128]{3,2,1,0:T(8,128)S(1)} %get-tuple-element.7.vk, f32[7,8,128]{2,1,0:T(8,128)S(1)} %get-tuple-element.8.mix, f32[192,128]{1,0:T(8,128)S(1)} %get-tuple-element.9.center), custom_call_target="tpu_custom_call" | custom-call | tf_op jit(solution)/shard_map/pallas_call | solution.py:576

commit v2 on v1

--- a/solution.py
+++ b/solution.py
@@ -8,10 +8,12 @@
 from jax.sharding import PartitionSpec as P
 
 ITERS = 3
+BATCH = 2
 MESH = pl.DeviceIdType.MESH
 EDGE = 16
 SLOT = 16
-STRIP, KSTRIP, EAST, NORTH, NEAST, NWEST, SCALE, ARRAYS = range(8, 16)
+RIM, KRIM, EAST, NORTH, NEAST, NWEST, SCALE, ARRAYS = range(8, 16)
+EXTRA = 5 * SLOT
 COUPLED = (EAST, NORTH, NEAST, NWEST, SCALE)
 FROM_S, FROM_N, FROM_SW, FROM_SE, FROM_NW, FROM_NE, FROM_W, FROM_E = range(8)
 
@@ -23,8 +25,8 @@
 def kernel(
     lat_count, lon_count,
     rhs, center_hbm, coup_hbm, land_hbm, partner_hbm, st, vk, mix, cen,
-    land, partner, strips, coefm, coefs, pack, packin, rowin, diagin, fold,
-    macc, red, redlon, redlat,
+    land, partner, strips, kstrip, beyond, coefm, coefs, pack, packin, rowin, diagin, fold,
+    macc, sacc, red, redlon, redlat,
     load_sem, send_sem, recv_sem, fold_ss, fold_rs, lon_ss, lon_rs, lat_ss, lat_rs,
 ):
     f32 = jnp.float32
@@ -32,7 +34,10 @@
     tiles = rows // 8
     first, last = 2, tiles + 1
     inner = tiles - 2
-    unroll = max(u for u in range(1, 12) if inner % u == 0)
+
+    def split(count, most):
+        return max(u for u in range(1, most + 1) if count % u == 0)
+
     la, lo = lax.axis_index("lat"), lax.axis_index("lon")
     lat_first, lat_last = la == 0, la == lat_count - 1
     not_first, not_last = la > 0, la < lat_count - 1
@@ -69,16 +74,12 @@
     for c in loads:
         c.wait()
 
-    inside_w = jnp.logical_and(place >= 3, place < 8)
-    inside_e = jnp.logical_and(place >= 8, place < 13)
-
-    def own_strip(arrays):
+    rim_lanes = [jnp.bitwise_and(lane - (SLOT * g - 3), cols - 1) < 12 for g in range(8)]
+
+    def rim(arrays):
         out = zero
         for g, x in enumerate(arrays):
-            mine = group == g
-            out = jnp.where(jnp.logical_and(mine, inside_w), roll(x, g * SLOT + 3), out)
-            out = jnp.where(jnp.logical_and(mine, inside_e),
-                            roll(x, (g * SLOT + 13) % cols), out)
+            out = jnp.where(rim_lanes[g], roll(x, g * SLOT + 3), out)
         return out
 
     def prep(t, carry):
@@ -94,21 +95,24 @@
                 v = st[m, rs, :] * d
                 st[m, rs, :] = v
                 vals.append(v)
-            s = own_strip(vals)
-            st[STRIP, rs, :] = s
-            k = own_strip([st[c, rs, :] for c in COUPLED[:4]] + [d])
-            st[KSTRIP, rs, :] = k
-            mine = lax.shift_right_logical(place, 2) == q
-            pe = jnp.where(mine, roll(s, (4 * q - 10) % cols), pe)
-            pw = jnp.where(mine, roll(s, (4 * q - 3) % cols), pw)
-            ke = jnp.where(mine, roll(k, (4 * q - 10) % cols), ke)
-            kw = jnp.where(mine, roll(k, (4 * q - 3) % cols), kw)
+            o = rim(vals)
+            st[RIM, rs, :] = o
+            k = rim([st[c, rs, :] for c in COUPLED[:4]] + [d])
+            st[KRIM, rs, :] = k
+            if q:
+                o, k = roll(o, 3 * q), roll(k, 3 * q)
+            here = jnp.logical_and(place >= 3 * q, place < 3 * q + 3)
+            after = jnp.logical_and(place >= 3 * q + 3, place < 3 * q + 6)
+            pe = jnp.where(here, o, pe)
+            pw = jnp.where(after, o, pw)
+            ke = jnp.where(here, k, ke)
+            kw = jnp.where(after, k, kw)
         pack[0, 0, t] = pe
         pack[0, 1, t] = ke
         pack[1, 0, t] = pw
         pack[1, 1, t] = kw
         return carry
-    lax.fori_loop(0, tiles // 4, prep, 0)
+    lax.fori_loop(0, tiles // 4, prep, 0, unroll=split(tiles // 4, 3))
 
     top, bottom = pl.ds(EDGE + rows - 3, 3), pl.ds(EDGE, 3)
 
@@ -119,7 +123,7 @@
 
     sides = [remote(pack.at[0], packin.at[0], FROM_W, (la, east)),
              remote(pack.at[1], packin.at[1], FROM_E, (la, west))]
-    pair = pl.ds(STRIP, 2)
+    pair = pl.ds(RIM, 2)
     low, high = pl.ds(5, 3), pl.ds(0, 3)
     up = [remote(st.at[:, top], rowin.at[0, :, low], FROM_S, (north, lo)),
           remote(st.at[pair, top], diagin.at[0, :, low], FROM_SW, (north, east)),
@@ -165,57 +169,56 @@
         for c in down:
             c.start()
 
-    for c in sides:
-        c.wait_recv()
-
-    def merge(t, carry):
-        for g in range(2):
-            fw, fe = packin[0, g, t], packin[1, g, t]
-            for q in range(4):
-                rs = at(first + t * 4 + q)
-                x = st[STRIP + g, rs, :]
-                x = jnp.where(place < 3, roll(fw, (-4 * q) % cols) if q else fw, x)
-                x = jnp.where(place > 12, roll(fe, 13 - 4 * q), x)
-                strips[0, g, rs, :] = x
+    def unfold(o, k, ow, kw, oe, ke):
+        def windows(x, w, e):
+            x = jnp.where(place < 8, x, roll(x, 10))
+            x = jnp.where(place < 3, w, x)
+            return jnp.where(place < 13, x, e)
+        ring = jnp.where(place == 7, roll(o, cols - 1), jnp.where(place == 8, roll(o, 11), 0.0))
+        return windows(o, ow, oe), ring, extras(windows(k, kw, ke), k)
+
+    def extras(x, k):
+        x = jnp.where(lane == EXTRA, roll(k, EXTRA + 3), x)
+        x = jnp.where(lane == EXTRA + 1, roll(k, EXTRA + 1 - 2 * SLOT + 3), x)
+        return jnp.where(lane == EXTRA + 2, roll(k, EXTRA + 2 - 3 * SLOT - 8), x)
+
+    def put_strip(rs, parts_):
+        strips[0, rs, :], beyond[rs, :], kstrip[rs, :] = parts_
+
+    def open_rims(t, carry):
+        rs = at(first + t)
+        put_strip(rs, unfold(st[RIM, rs, :], st[KRIM, rs, :], zero, zero, zero, zero))
         return carry
-    lax.fori_loop(0, tiles // 4, merge, 0)
-
-    def lateral(x, s, g):
-        xe = jnp.where(lane == cols - 1, roll(s, lax.rem(2 * cols - 14 - SLOT * g, cols)),
-                       roll(x, cols - 1))
-        xw = jnp.where(lane == 0, roll(s, lax.rem(2 * cols - 2 - SLOT * g, cols)), roll(x, 1))
-        return xe, xw
 
     def main_coefs(tile):
         rs = at(tile)
         start = tile * 8
         below = pl.ds(start - 1, 8)
         above = pl.ds(start + 1, 8)
-        k = strips[0, 1, rs, :]
-
-        def from_west(a, g):
-            return jnp.where(lane == 0, roll(k, cols - 2 - SLOT * g), roll(st[a, rs, :], 1))
         d, dn = st[SCALE, rs, :], st[SCALE, above, :]
         ds_ = st[SCALE, below, :]
         coefm[0, rs, :] = d * st[EAST, rs, :]
-        coefm[1, rs, :] = d * from_west(EAST, 0)
+        coefm[1, rs, :] = d * roll(st[EAST, rs, :], 1)
         coefm[2, rs, :] = ds_ * st[NORTH, below, :]
         coefm[3, rs, :] = ds_ * st[NEAST, below, :]
         coefm[4, rs, :] = ds_ * st[NWEST, below, :]
         coefm[5, rs, :] = dn * st[NORTH, rs, :]
-        coefm[6, rs, :] = dn * jnp.where(lane == cols - 1, roll(k, cols - 14 - SLOT * 3),
-                                         roll(st[NWEST, rs, :], cols - 1))
-        coefm[7, rs, :] = dn * from_west(NEAST, 2)
+        coefm[6, rs, :] = dn * roll(st[NWEST, rs, :], cols - 1)
+        coefm[7, rs, :] = dn * roll(st[NEAST, rs, :], 1)
 
     def strip_coefs(tile):
         rs = at(tile)
         start = tile * 8
-        here = strips[0, 1, rs, :]
-        below = strips[0, 1, pl.ds(start - 1, 8), :]
-        above = strips[0, 1, pl.ds(start + 1, 8), :]
+        here = kstrip[rs, :]
+        below = kstrip[pl.ds(start - 1, 8), :]
+        above = kstrip[pl.ds(start + 1, 8), :]
 
         def spread(x, g, shift=0):
             where = jnp.bitwise_and(place + (g * SLOT + shift), cols - 1)
+            if shift < 0:
+                where = jnp.where(place == 8, EXTRA + g // 2, where)
+            if shift > 0:
+                where = jnp.where(place == 7, EXTRA + 2, where)
             return jnp.take_along_axis(x, where, axis=1, mode="promise_in_bounds")
         d, ds_, dn = spread(here, 4), spread(below, 4), spread(above, 4)
         coefs[0, rs, :] = d * spread(here, 0)
@@ -226,12 +229,16 @@
         coefs[5, rs, :] = dn * spread(here, 1)
         coefs[6, rs, :] = dn * spread(here, 3, 1)
         coefs[7, rs, :] = dn * spread(here, 2, -1)
+        edge = jnp.logical_or(jnp.logical_and(place >= 3, place < 6),
+                              jnp.logical_and(place >= 10, place < 13))
+        used = jnp.logical_and(edge, d > 0.0)
+        coefs[8, rs, :] = jnp.where(used, 1.0 / jnp.where(used, d, 1.0), 0.0)
 
     def all_coefs(t, carry):
         main_coefs(first + t)
-        strip_coefs(first + t)
         return carry
-    lax.fori_loop(0, tiles, all_coefs, 0, unroll=4)
+    lax.fori_loop(0, tiles, all_coefs, 0, unroll=split(tiles, 24))
+    lax.fori_loop(0, tiles, open_rims, 0, unroll=split(tiles, 24))
 
     def parts(x, xe, xw, c):
         cross = c[0] * xe + c[1] * xw
@@ -250,35 +257,21 @@
 
     def strip_parts(k, tile):
         rs = at(tile)
-        x = strips[k, 0, rs, :]
-        return parts(x, roll(x, cols - 1), roll(x, 1), [coefs[q, rs, :] for q in range(8)])
+        x = strips[k, rs, :]
+        xe, xw = roll(x, cols - 1), roll(x, 1)
+        if k == 0:
+            near = beyond[rs, :]
+            xe, xw = jnp.where(place == 7, near, xe), jnp.where(place == 8, near, xw)
+        return x, parts(x, xe, xw, [coefs[q, rs, :] for q in range(8)])
 
     def member_parts(k, g, tile, c=None):
         rs = at(tile)
         x = source(k, g, rs)
-        xe, xw = lateral(x, strips[k, 0, rs, :], g)
         if c is None:
             c = [coefm[q, rs, :] for q in range(8)]
-        return x, parts(x, xe, xw, c)
-
-    for k in range(ITERS - 1):
-        cross, upper, lower = strip_parts(k, first)
-
-        def strip_step(b, carry):
-            sofar, u_old, d_old = carry
-            for u in range(unroll):
-                tile = first + 1 + b * unroll + u
-                cross, upper, lower = strip_parts(k, tile)
-                strips[k + 1, 0, at(tile - 1), :] = sofar + shift_up(u_old, upper)
-                sofar, u_old, d_old = cross + shift_down(d_old, lower), upper, lower
-            return sofar, u_old, d_old
-        sofar, u_old, d_old = lax.fori_loop(
-            0, inner // unroll, strip_step, (cross + shift_down(zero, lower), upper, lower))
-        cross, upper, lower = strip_parts(k, last)
-        strips[k + 1, 0, at(last - 1), :] = sofar + shift_up(u_old, upper)
-        strips[k + 1, 0, at(last), :] = cross + shift_down(d_old, lower) + shift_up(upper, zero)
-
-    batch = 2
+        return x, parts(x, roll(x, cols - 1), roll(x, 1), c)
+
+    batch = BATCH
     for k in range(ITERS):
         def sweep(p, carry):
             gs = [p * batch + i for i in range(batch)]
@@ -287,24 +280,22 @@
                 _, (cross, upper, lower) = member_parts(k, g, first)
                 state.append((cross + shift_down(zero, lower), upper, lower, zero, zero, zero))
 
-            def step(b, state):
+            def step(t, state):
                 state = list(state)
-                for u in range(unroll):
-                    tile = first + 1 + b * unroll + u
-                    rs = at(tile)
-                    c = [coefm[q, rs, :] for q in range(8)]
-                    weight = cen[at(tile - first), :]
-                    for i, g in enumerate(gs):
-                        sofar, u_old, d_old, w_old, acc0, acc1 = state[i]
-                        x, (cross, upper, lower) = member_parts(k, g, tile, c)
-                        out = sofar + shift_up(u_old, upper)
-                        vk[k, g, at(tile - 1), :] = out
-                        acc1 = acc1 + w_old * out
-                        w = weight * x
-                        acc0 = acc0 + w * x
-                        state[i] = (cross + shift_down(d_old, lower), upper, lower, w, acc0, acc1)
+                tile = first + 1 + t
+                c = [coefm[q, at(tile), :] for q in range(8)]
+                weight = cen[at(tile - first), :]
+                for i, g in enumerate(gs):
+                    sofar, u_old, d_old, w_old, acc0, acc1 = state[i]
+                    x, (cross, upper, lower) = member_parts(k, g, tile, c)
+                    out = sofar + shift_up(u_old, upper)
+                    vk[k, g, at(tile - 1), :] = out
+                    acc1 = acc1 + w_old * out
+                    w = weight * x
+                    acc0 = acc0 + w * x
+                    state[i] = (cross + shift_down(d_old, lower), upper, lower, w, acc0, acc1)
                 return tuple(state)
-            state = lax.fori_loop(0, inner // unroll, step, tuple(state))
+            state = lax.fori_loop(0, inner, step, tuple(state), unroll=split(inner, 22))
             for i, g in enumerate(gs):
                 sofar, u_old, d_old, w_old, acc0, acc1 = state[i]
                 _, (cross, upper, lower) = member_parts(k, g, last)
@@ -316,39 +307,54 @@
             return carry
         lax.fori_loop(0, members // batch, sweep, 0)
 
+    for c in sides:
+        c.wait_recv()
+
+    def merge(t, carry):
+        fw, fe = [packin[0, g, t] for g in range(2)], [packin[1, g, t] for g in range(2)]
+        for q in range(4):
+            rs = at(first + t * 4 + q)
+            for g, ref in enumerate((strips.at[0], kstrip)):
+                x = ref[rs, :]
+                keep = lane < EXTRA if g else lane >= 0
+                x = jnp.where(jnp.logical_and(place < 3, keep),
+                              roll(fw[g], (-3 * q) % cols) if q else fw[g], x)
+                x = jnp.where(jnp.logical_and(place > 12, keep), roll(fe[g], 10 - 3 * q), x)
+                ref[rs, :] = x
+        return carry
+    lax.fori_loop(0, tiles // 4, merge, 0, unroll=split(tiles // 4, 6))
+
+    def take_rows(side, tile, seen):
+        rs = at(tile)
+
+        def clean(x):
+            return jnp.where(seen, x, 0.0)
+        for a in range(ARRAYS):
+            if a not in (RIM, KRIM):
+                st[a, rs, :] = clean(rowin[side, a])
+        o, k = clean(rowin[side, RIM]), clean(rowin[side, KRIM])
+        ow, kw = (clean(diagin[2 * side, i]) for i in range(2))
+        oe, ke = (roll(clean(diagin[2 * side + 1, i]), 10) for i in range(2))
+        put_strip(rs, unfold(o, k, ow, kw, oe, ke))
+
     @pl.when(not_first)
     def _():
-        for s in (FROM_S, FROM_SW, FROM_SE):
-            up[s if s == FROM_S else s - FROM_SW + 1].wait_recv()
-        rs = at(first - 1)
-        for a in range(ARRAYS):
-            if a not in (STRIP, KSTRIP):
-                st[a, rs, :] = rowin[0, a]
-        for g in range(2):
-            x = rowin[0, STRIP + g]
-            x = jnp.where(place < 3, roll(diagin[0, g], cols - 10), x)
-            strips[0, g, rs, :] = jnp.where(place > 12, roll(diagin[1, g], 10), x)
+        for c in up:
+            c.wait_recv()
+        take_rows(0, first - 1, sub > 4)
 
     @pl.when(lat_first)
     def _():
         rs = at(first - 1)
         for a in range(ARRAYS):
             st[a, rs, :] = zero
-        for g in range(2):
-            strips[0, g, rs, :] = zero
+        put_strip(rs, (zero, zero, zero))
 
     @pl.when(not_last)
     def _():
         for c in down:
             c.wait_recv()
-        rs = at(last + 1)
-        for a in range(ARRAYS):
-            if a not in (STRIP, KSTRIP):
-                st[a, rs, :] = rowin[1, a]
-        for g in range(2):
-            x = rowin[1, STRIP + g]
-            x = jnp.where(place < 3, roll(diagin[2, g], cols - 10), x)
-            strips[0, g, rs, :] = jnp.where(place > 12, roll(diagin[3, g], 10), x)
+        take_rows(1, last + 1, sub < 3)
 
     @pl.when(lat_last)
     def _():
@@ -373,11 +379,13 @@
         views = {s: view(s) for s in (-1, 0, 1)}
         shifts = {EAST: -1, NEAST: -1, NWEST: 1}
         ghost = [zero, zero]
+        blocks = []
         for i, a in enumerate(fold_arrays):
             slots, where, within, where_s, (far, near, back) = views[shifts.get(a, 0)]
-            chunks = [fold[s, i] for s in slots]
+            chunks = [jnp.where(sub < 3, fold[s, i], 0.0) for s in slots]
             block = jnp.where(within, take(chunks[1], where), take(chunks[2], where))
             st[a, rs, :] = block
+            blocks.append(block)
             x = jnp.where(back, take(chunks[2], where_s), take(chunks[3], where_s))
             x = jnp.where(near, take(chunks[1], where_s), x)
             x = jnp.where(far, take(chunks[0], where_s), x)
@@ -386,69 +394,91 @@
             if a == NORTH:
                 end = pl.ds(EDGE + rows - 1, 1)
                 st[NORTH, end, :] = 0.5 * (st[NORTH, end, :] + block[2:3, :])
-                mixed = 0.5 * (strips[0, 1, end, :] + x[2:3, :])
-                g1 = group[0:1, :]
-                dropped = jnp.logical_or(g1 == 2, g1 == 3)
-                strips[0, 1, end, :] = jnp.where(
-                    dropped, 0.0, jnp.where(g1 == 1, mixed, strips[0, 1, end, :]))
+                mixed = 0.5 * (kstrip[end, :] + x[2:3, :])
+                g1, l1 = group[0:1, :], lane[0:1, :]
+                dropped = jnp.logical_or(jnp.logical_or(g1 == 2, g1 == 3),
+                                         jnp.logical_or(l1 == EXTRA + 1, l1 == EXTRA + 2))
+                kstrip[end, :] = jnp.where(
+                    dropped, 0.0, jnp.where(g1 == 1, mixed, kstrip[end, :]))
                 st[NEAST, end, :] = jnp.zeros((1, cols), f32)
                 st[NWEST, end, :] = jnp.zeros((1, cols), f32)
-        for s in range(2):
-            strips[0, s, rs, :] = ghost[s]
+        o, k = rim(blocks[:members]), rim(blocks[members:])
+        ring = unfold(o, k, zero, zero, zero, zero)[1]
+        put_strip(rs, (ghost[0], ring, extras(ghost[1], k)))
 
     for tile in (first - 1, first, last, last + 1):
         main_coefs(tile)
-        strip_coefs(tile)
+
+    def edge_coefs(t, carry):
+        strip_coefs(first - 1 + t)
+        return carry
+    lax.fori_loop(0, tiles + 2, edge_coefs, 0, unroll=split(tiles + 2, 26))
 
     def join(lo_parts, mid, hi_parts):
         out = mid[0]
         out = out + shift_down(zero if lo_parts is None else lo_parts[2], mid[2])
         return out + shift_up(mid[1], zero if hi_parts is None else hi_parts[1])
 
-    for k in range(ITERS - 1):
-        b = [strip_parts(k, t) for t in (first - 1, first, first + 1)]
-        t = [strip_parts(k, t) for t in (last - 1, last, last + 1)]
-        strips[k + 1, 0, at(first - 1), :] = join(None, b[0], b[1])
-        strips[k + 1, 0, at(first), :] = join(b[0], b[1], b[2])
-        strips[k + 1, 0, at(last), :] = join(t[0], t[1], t[2])
-        strips[k + 1, 0, at(last + 1), :] = join(t[1], t[2], None)
     for k in range(ITERS):
-        def band(p, carry):
-            for i in range(batch):
-                g = p * batch + i
-                b = [member_parts(k, g, t) for t in (first - 1, first, first + 1)]
-                t = [member_parts(k, g, t) for t in (last - 1, last, last + 1)]
-                if k + 1 < ITERS:
-                    vk[k, g, at(first - 1), :] = join(None, b[0][1], b[1][1])
-                    vk[k, g, at(last + 1), :] = join(t[1][1], t[2][1], None)
-                acc0, acc1 = macc[2 * k, g], macc[2 * k + 1, g]
-                for tile, three in ((first, b), (last, t)):
-                    out = join(three[0][1], three[1][1], three[2][1])
-                    vk[k, g, at(tile), :] = out
-                    x = three[1][0]
-                    w = cen[at(tile - first), :] * x
-                    acc0 = acc0 + w * x
-                    acc1 = acc1 + w * out
-                macc[2 * k, g] = acc0
-                macc[2 * k + 1, g] = acc1
+        _, (cross, upper, lower) = strip_parts(k, first - 1)
+
+        def strip_step(t, carry):
+            sofar, u_old, d_old, w_old, acc0, acc1 = carry
+            tile = first + t
+            x, (cross, upper, lower) = strip_parts(k, tile)
+            out = sofar + shift_up(u_old, upper)
+            strips[k + 1, at(tile - 1), :] = out
+            acc1 = acc1 + w_old * out
+            w_old = coefs[8, at(tile), :] * x
+            acc0 = acc0 + w_old * x
+            return cross + shift_down(d_old, lower), upper, lower, w_old, acc0, acc1
+        sofar, u_old, d_old, w_old, acc0, acc1 = lax.fori_loop(
+            0, tiles, strip_step,
+            (cross + shift_down(zero, lower), upper, lower, zero, zero, zero),
+            unroll=split(tiles, 24))
+        _, (cross, upper, lower) = strip_parts(k, last + 1)
+        out = sofar + shift_up(u_old, upper)
+        strips[k + 1, at(last), :] = out
+        strips[k + 1, at(last + 1), :] = cross + shift_down(d_old, lower) + shift_up(upper, zero)
+        sacc[2 * k] = acc0
+        sacc[2 * k + 1] = acc1 + w_old * out
+
+        def band(g, carry):
+            b = [member_parts(k, g, t) for t in (first - 1, first, first + 1)]
+            t = [member_parts(k, g, t) for t in (last - 1, last, last + 1)]
+            if k + 1 < ITERS:
+                vk[k, g, at(first - 1), :] = join(None, b[0][1], b[1][1])
+                vk[k, g, at(last + 1), :] = join(t[1][1], t[2][1], None)
+            acc0, acc1 = macc[2 * k, g], macc[2 * k + 1, g]
+            for tile, three in ((first, b), (last, t)):
+                out = join(three[0][1], three[1][1], three[2][1])
+                vk[k, g, at(tile), :] = out
+                x = three[1][0]
+                w = cen[at(tile - first), :] * x
+                acc0 = acc0 + w * x
+                acc1 = acc1 + w * out
+            macc[2 * k, g] = acc0
+            macc[2 * k + 1, g] = acc1
             return carry
-        lax.fori_loop(0, members // batch, band, 0)
-
+        lax.fori_loop(0, members, band, 0, unroll=members)
+
+    def column_sum(x):
+        for s in (4, 2, 1):
+            x = x + roll(x, s, 0)
+        return x
     row = zero
     for i in range(2 * ITERS):
         total = macc[i, :, 0, :]
         for s in range(1, 8):
             total = total + macc[i, :, s, :]
+        total = jnp.where(jnp.logical_and(lane > 2, lane < cols - 3), total, 0.0)
+        total = total + jnp.where(group == sub, column_sum(sacc[i]), 0.0)
         total = jnp.sum(total, axis=1, keepdims=True)
         row = jnp.where(lane == 8 * i + sub, total, row)
 
-    def column_sum(x):
-        for s in (4, 2, 1):
-            x = x + roll(x, s, 0)
-        return x
     row = column_sum(row)
 
-    def reduce(value, slot, recv, me, ss, rs, count, dev):
+    def reduce(value, slot, recv, me, ss, rs, count, dev, between=None):
         red[slot] = value
         cps = [
             pltpu.make_async_remote_copy(
@@ -459,6 +489,8 @@
         for c in cps:
             c.start()
         recv[me] = value
+        if between:
+            between()
         for c in cps:
             c.wait_recv()
         out = recv[0, pl.ds(0, 1), :]
@@ -466,8 +498,22 @@
             out = out + recv[d, pl.ds(0, 1), :]
         return jnp.broadcast_to(out, (8, cols)), cps
 
+    outer = jnp.logical_or(lane < 3, lane > cols - 4)
+
+    def close_rims():
+        for k in range(1, ITERS + 1):
+            def close(t, carry):
+                rs = at(first + t)
+                x = strips[k, rs, :]
+                x = jnp.where(place < 3, roll(x, cols - 10), x)
+                for m in range(members):
+                    edge = roll(x, (cols - 3 - SLOT * m) % cols)
+                    vk[k - 1, m, rs, :] = jnp.where(outer, edge, vk[k - 1, m, rs, :])
+                return carry
+            lax.fori_loop(0, tiles, close, 0, unroll=split(tiles, 8))
+
     row, c1 = reduce(row, 0, redlon, lo, lon_ss, lon_rs, lon_count,
-                     lambda d: (la, lax.rem(lo + d, lon_count)))
+                     lambda d: (la, lax.rem(lo + d, lon_count)), close_rims)
     row, c2 = reduce(row, 1, redlat, la, lat_ss, lat_rs, lat_count,
                      lambda d: (lax.rem(la + d, lat_count), lo))
 
@@ -552,15 +598,18 @@
         scratch_shapes=[
             pltpu.VMEM((rows, cols), jnp.int32),
             pltpu.SMEM((1, cols), jnp.int32),
-            pltpu.VMEM((ITERS, 2, high, cols), f32),
+            pltpu.VMEM((ITERS + 1, high, cols), f32),
+            pltpu.VMEM((high, cols), f32),
+            pltpu.VMEM((high, cols), f32),
             pltpu.VMEM((8, high, cols), f32),
-            pltpu.VMEM((8, high, cols), f32),
+            pltpu.VMEM((9, high, cols), f32),
             pltpu.VMEM((2, 2, tiles // 4, 8, cols), f32),
             pltpu.VMEM((2, 2, tiles // 4, 8, cols), f32),
             pltpu.VMEM((2, ARRAYS, 8, cols), f32),
             pltpu.VMEM((4, 2, 8, cols), f32),
             pltpu.VMEM((lon_count, folded, 8, cols), f32),
             pltpu.VMEM((2 * ITERS, members, 8, cols), f32),
+            pltpu.VMEM((2 * ITERS, 8, cols), f32),
             pltpu.VMEM((2, 8, cols), f32),
             pltpu.VMEM((lon_count, 8, cols), f32),
             pltpu.VMEM((lat_count, 8, cols), f32),

time: 29.9 us -> 23.6 us (0.79)
  Pallas kernels: 29.1 us -> 22.8 us
    pallas_call x1, Pallas kernels: 27.8 us -> 21.5 us  [body(): pl.pallas_call(functools.partial(kernel, lat_count, lon_count), out_shape...]
where the time goes in v2:
time: 23.6 us; the launch traced here: 23.4 us
  Pallas kernels  22.8 us (97%)
  between operations  0.64 us (3%)
    pallas_call x1, Pallas kernels, body(): pl.pallas_call(functools.partial(kernel, lat_count, lon_count), out_shape...  21.5 us
    pallas_call x1, Pallas kernels, body(): pl.pallas_call(finish, out_shape=(shape, shape), in_specs=[vmem] * 4, out...  1.31 us

profile of v2, /device:TPU:0, one launch (start us, length us, event | category | flops | bytes accessed | tf_op | source)
XLA Modules:
  0.0 23.4 jit_solution(199540437934557953)
XLA Ops:
  0.6 21.5 %shard_map.68 = (f32[15,224,128]{2,1,0:T(8,128)S(1)}, f32[3,8,224,128]{3,2,1,0:T(8,128)S(1)}, f32[7,8,128]{2,1,0:T(8,128)S(1)}, f32[192,128]{1,0:T(8,128)S(1)}) custom-call(f32[8,192,128]{2,1,0:T(8,128)} %rhs.1, f32[192,128]{1,0:T(8,128)} %center_hbm.1, f32[4,192,128]{2,1,0:T(8,128)} %coup_hbm.1, s32[192,128]{1,0:T(8,128)} %land_hbm.1, s32[8,128]{1,0:T(8,128)} %bitcast.1), custom_call_target="tpu_custom_call" | custom-call | tf_op jit(solution)/shard_map/pallas_call | solution.py:590
  22.1 1.3 %shard_map.69 = (f32[8,192,128]{2,1,0:T(8,128)}, f32[8,192,128]{2,1,0:T(8,128)}) custom-call(f32[15,224,128]{2,1,0:T(8,128)S(1)} %get-tuple-element.6.st, f32[3,8,224,128]{3,2,1,0:T(8,128)S(1)} %get-tuple-element.7.vk, f32[7,8,128]{2,1,0:T(8,128)S(1)} %get-tuple-element.8.mix, f32[192,128]{1,0:T(8,128)S(1)} %get-tuple-element.9.center), custom_call_target="tpu_custom_call" | custom-call | tf_op jit(solution)/shard_map/pallas_call | solution.py:625

commit v3 on v2

--- a/solution.py
+++ b/solution.py
@@ -25,7 +25,7 @@
 def kernel(
     lat_count, lon_count,
     rhs, center_hbm, coup_hbm, land_hbm, partner_hbm, st, vk, mix, cen,
-    land, partner, strips, kstrip, beyond, coefm, coefs, pack, packin, rowin, diagin, fold,
+    land, partner, strips, kstrip, beyond, coefm, coefs, wide, pack, packin, rowin, diagin, fold,
     macc, sacc, red, redlon, redlat,
     load_sem, send_sem, recv_sem, fold_ss, fold_rs, lon_ss, lon_rs, lat_ss, lat_rs,
 ):
@@ -53,26 +53,37 @@
         start = tile * 8
         return pl.ds(start if isinstance(start, int) else pl.multiple_of(start, 8), 8)
 
-    own = pl.ds(EDGE, rows)
-    loads = [
-        pltpu.make_async_copy(center_hbm, cen, load_sem.at[0]),
-        pltpu.make_async_copy(land_hbm, land, load_sem.at[1]),
-        pltpu.make_async_copy(partner_hbm.at[pl.ds(0, 1)], partner, load_sem.at[2]),
-        pltpu.make_async_copy(coup_hbm, st.at[pl.ds(EAST, 4), own], load_sem.at[3]),
-        pltpu.make_async_copy(rhs, st.at[pl.ds(0, members), own], load_sem.at[4]),
-    ]
+    loads = []
+    for i, (start, size) in enumerate(((0, 8), (rows - 8, 8), (8, rows - 16))):
+        rs, own = pl.ds(start, size), pl.ds(EDGE + start, size)
+        loads += [
+            pltpu.make_async_copy(center_hbm.at[rs], cen.at[rs], load_sem.at[i, 0]),
+            pltpu.make_async_copy(land_hbm.at[rs], land.at[rs], load_sem.at[i, 1]),
+            pltpu.make_async_copy(coup_hbm.at[:, rs], st.at[pl.ds(EAST, 4), own],
+                                  load_sem.at[i, 2]),
+            pltpu.make_async_copy(rhs.at[:, rs], st.at[pl.ds(0, members), own],
+                                  load_sem.at[i, 3]),
+        ]
+    loads.append(pltpu.make_async_copy(partner_hbm.at[pl.ds(0, 1)], partner, load_sem.at[0, 4]))
     for c in loads:
         c.start()
 
     barrier = pltpu.get_barrier_semaphore()
     partners = [(la, lax.rem(lo + d, lon_count)) for d in range(1, lon_count)]
     partners += [(lax.rem(la + d, lat_count), lo) for d in range(1, lat_count)]
-    partners += [(north, east), (north, west), (south, east), (south, west)]
     for p in partners:
         pl.semaphore_signal(barrier, inc=1, device_id=p, device_id_type=MESH)
 
-    for c in loads:
-        c.wait()
+    @pl.when(not_last)
+    def _():
+        for p in ((north, east), (north, west)):
+            pl.semaphore_signal(barrier, inc=1, device_id=p, device_id_type=MESH)
+
+    @pl.when(not_first)
+    def _():
+        for p in ((south, east), (south, west)):
+            pl.semaphore_signal(barrier, inc=1, device_id=p, device_id_type=MESH)
+    arrivals = (len(partners) + 2 * jnp.where(not_last, 1, 0) + 2 * jnp.where(not_first, 1, 0))
 
     rim_lanes = [jnp.bitwise_and(lane - (SLOT * g - 3), cols - 1) < 12 for g in range(8)]
 
@@ -82,37 +93,38 @@
             out = jnp.where(rim_lanes[g], roll(x, g * SLOT + 3), out)
         return out
 
+    def prep_tile(tile):
+        rs = at(tile)
+        near = at(tile - first)
+        d = land[near, :].astype(f32) / cen[near, :]
+        st[SCALE, rs, :] = d
+        vals = []
+        for m in range(members):
+            v = st[m, rs, :] * d
+            st[m, rs, :] = v
+            vals.append(v)
+        st[RIM, rs, :] = rim(vals)
+        st[KRIM, rs, :] = rim([st[c, rs, :] for c in COUPLED[:4]] + [d])
+
     def prep(t, carry):
-        pe, pw, ke, kw = zero, zero, zero, zero
+        prep_tile(first + 1 + t)
+        return carry
+
+    def fill(t, carry):
+        packs = [zero] * 4
         for q in range(4):
-            tile = first + t * 4 + q
-            rs = at(tile)
-            near = at(tile - first)
-            d = land[near, :].astype(f32) / cen[near, :]
-            st[SCALE, rs, :] = d
-            vals = []
-            for m in range(members):
-                v = st[m, rs, :] * d
-                st[m, rs, :] = v
-                vals.append(v)
-            o = rim(vals)
-            st[RIM, rs, :] = o
-            k = rim([st[c, rs, :] for c in COUPLED[:4]] + [d])
-            st[KRIM, rs, :] = k
-            if q:
-                o, k = roll(o, 3 * q), roll(k, 3 * q)
+            rs = at(first + t * 4 + q)
             here = jnp.logical_and(place >= 3 * q, place < 3 * q + 3)
             after = jnp.logical_and(place >= 3 * q + 3, place < 3 * q + 6)
-            pe = jnp.where(here, o, pe)
-            pw = jnp.where(after, o, pw)
-            ke = jnp.where(here, k, ke)
-            kw = jnp.where(after, k, kw)
-        pack[0, 0, t] = pe
-        pack[0, 1, t] = ke
-        pack[1, 0, t] = pw
-        pack[1, 1, t] = kw
+            for g in range(2):
+                x = st[RIM + g, rs, :]
+                x = roll(x, 3 * q) if q else x
+                packs[g] = jnp.where(here, x, packs[g])
+                packs[2 + g] = jnp.where(after, x, packs[2 + g])
+        for side in range(2):
+            for g in range(2):
+                pack[side, g, t] = packs[2 * side + g]
         return carry
-    lax.fori_loop(0, tiles // 4, prep, 0, unroll=split(tiles // 4, 3))
 
     top, bottom = pl.ds(EDGE + rows - 3, 3), pl.ds(EDGE, 3)
 
@@ -131,40 +143,89 @@
     down = [remote(st.at[:, bottom], rowin.at[1, :, high], FROM_N, (south, lo)),
             remote(st.at[pair, bottom], diagin.at[2, :, high], FROM_NW, (south, east)),
             remote(st.at[pair, bottom], diagin.at[3, :, high], FROM_NE, (south, west))]
-    folds = [
-        pltpu.make_async_remote_copy(
-            src_ref=fold.at[0, :, high], dst_ref=fold.at[d, :, high],
-            send_sem=fold_ss.at[d], recv_sem=fold_rs.at[d],
-            device_id=(la, lax.rem(lo + d, lon_count)), device_id_type=MESH)
-        for d in range(1, lon_count)
-    ]
     fold_arrays = list(range(members)) + list(COUPLED)
-
-    pl.semaphore_wait(barrier, len(partners))
-    for c in sides:
-        c.start()
+    fold_picks = {a: (0, 1, 2) for a in range(members)}
+    fold_picks.update({EAST: (0, 1), NORTH: (1, 2, 0), NEAST: (1, 2), NWEST: (1, 2), SCALE: (0, 1)})
+    fold_start = [0]
+    for a in fold_arrays:
+        fold_start.append(fold_start[-1] + len(fold_picks[a]))
+    sent = pl.ds(0, fold_start[-1])
+    mate = lo + 1 - 2 * lax.rem(lo, 2)
+    half = lon_count // 2
+
+    def fold_copy(sender, slot, dev):
+        return pltpu.make_async_remote_copy(
+            src_ref=fold.at[sender, sent], dst_ref=fold.at[sender, sent],
+            send_sem=fold_ss.at[slot], recv_sem=fold_rs.at[slot],
+            device_id=(la, dev), device_id_type=MESH)
+    folds = [fold_copy(lo, 0, mate)]
+    folds += [fold_copy(lo, j, lax.rem(lo + 2 * j, lon_count)) for j in range(1, half)]
+    relays = [fold_copy(lax.rem(lo + lon_count - 2 * j, lon_count), half + j, mate)
+              for j in range(1, half)]
+
+    for c in loads[:8]:
+        c.wait()
+    prep_tile(first)
+    prep_tile(last)
+
+    late = lo >= half
+    send_first = jnp.logical_and(lat_last, late)
 
     @pl.when(lat_last)
     def _():
         end = EDGE + rows - 1
         for i, a in enumerate(fold_arrays):
-            if a == NORTH:
-                picks = (end - 1, end - 2, end)
-            elif a in (NEAST, NWEST):
-                picks = (end - 1, end - 2, end - 2)
-            else:
-                picks = (end, end - 1, end - 2)
-            for g, r in enumerate(picks):
-                fold[0, i, pl.ds(g, 1), :] = st[a, pl.ds(r, 1), :]
-        for c in folds:
+            for g, r in enumerate(fold_picks[a]):
+                fold[lo, pl.ds(fold_start[i] + g, 1), :] = st[a, pl.ds(end - r, 1), :]
+        for i in range(fold_start[-1], fold.shape[1]):
+            fold[lo, pl.ds(i, 1), :] = jnp.zeros((1, cols), f32)
+
+    def send_folds():
+        if lat_count > 1:
+            for c in down:
+                c.start()
+        for c in folds[half // 2:] + folds[:half // 2]:
             c.start()
+
+    @pl.when(send_first)
+    def _():
+        pl.semaphore_wait(barrier, arrivals)
+        send_folds()
+
+    for c in loads[8:]:
+        c.wait()
+    lax.fori_loop(0, inner, prep, 0, unroll=split(inner, 11))
+    lax.fori_loop(0, tiles // 4, fill, 0, unroll=split(tiles // 4, 6))
+
+    @pl.when(jnp.logical_not(send_first))
+    def _():
+        pl.semaphore_wait(barrier, arrivals)
+
+    send_later = jnp.logical_and(lat_last, jnp.logical_not(late))
+
+    @pl.when(send_later)
+    def _():
+        if lat_count > 1:
+            for c in down:
+                c.start()
+        for c in folds[:half // 2:-1]:
+            c.start()
+
+    sides[1].start()
+
+    @pl.when(send_later)
+    def _():
+        for c in folds[:1] + folds[half // 2:0:-1]:
+            c.start()
+
+    sides[0].start()
 
     @pl.when(not_last)
     def _():
         for c in up:
             c.start()
 
-    @pl.when(not_first)
+    @pl.when(jnp.logical_and(not_first, not_last))
     def _():
         for c in down:
             c.start()
@@ -206,33 +267,41 @@
         coefm[6, rs, :] = dn * roll(st[NWEST, rs, :], cols - 1)
         coefm[7, rs, :] = dn * roll(st[NEAST, rs, :], 1)
 
-    def strip_coefs(tile):
+    def spread_tile(tile):
         rs = at(tile)
-        start = tile * 8
-        here = kstrip[rs, :]
-        below = kstrip[pl.ds(start - 1, 8), :]
-        above = kstrip[pl.ds(start + 1, 8), :]
-
-        def spread(x, g, shift=0):
+        x = kstrip[rs, :]
+
+        def spread(g, shift=0):
             where = jnp.bitwise_and(place + (g * SLOT + shift), cols - 1)
             if shift < 0:
                 where = jnp.where(place == 8, EXTRA + g // 2, where)
             if shift > 0:
                 where = jnp.where(place == 7, EXTRA + 2, where)
             return jnp.take_along_axis(x, where, axis=1, mode="promise_in_bounds")
-        d, ds_, dn = spread(here, 4), spread(below, 4), spread(above, 4)
-        coefs[0, rs, :] = d * spread(here, 0)
-        coefs[1, rs, :] = d * spread(here, 0, -1)
-        coefs[2, rs, :] = ds_ * spread(below, 1)
-        coefs[3, rs, :] = ds_ * spread(below, 2)
-        coefs[4, rs, :] = ds_ * spread(below, 3)
-        coefs[5, rs, :] = dn * spread(here, 1)
-        coefs[6, rs, :] = dn * spread(here, 3, 1)
-        coefs[7, rs, :] = dn * spread(here, 2, -1)
+        d = spread(4)
+        wide[0, rs, :] = d
+        for g in range(1, 4):
+            wide[g, rs, :] = spread(g)
+        coefs[0, rs, :] = d * spread(0)
+        coefs[1, rs, :] = d * spread(0, -1)
+        coefs[6, rs, :] = spread(3, 1)
+        coefs[7, rs, :] = spread(2, -1)
         edge = jnp.logical_or(jnp.logical_and(place >= 3, place < 6),
                               jnp.logical_and(place >= 10, place < 13))
         used = jnp.logical_and(edge, d > 0.0)
         coefs[8, rs, :] = jnp.where(used, 1.0 / jnp.where(used, d, 1.0), 0.0)
+
+    def strip_coefs(tile):
+        rs = at(tile)
+        start = tile * 8
+        below = pl.ds(start - 1, 8)
+        above = pl.ds(start + 1, 8)
+        ds_, dn = wide[0, below, :], wide[0, above, :]
+        for g in range(1, 4):
+            coefs[1 + g, rs, :] = ds_ * wide[g, below, :]
+        coefs[5, rs, :] = dn * wide[1, rs, :]
+        coefs[6, rs, :] = dn * coefs[6, rs, :]
+        coefs[7, rs, :] = dn * coefs[7, rs, :]
 
     def all_coefs(t, carry):
         main_coefs(first + t)
@@ -307,6 +376,76 @@
             return carry
         lax.fori_loop(0, members // batch, sweep, 0)
 
+    @pl.when(lat_last)
+    def _():
+        for c in folds[1:]:
+            c.wait_recv()
+        for c in relays:
+            c.start()
+
+    def join(lo_parts, mid, hi_parts):
+        out = mid[0]
+        out = out + shift_down(zero if lo_parts is None else lo_parts[2], mid[2])
+        return out + shift_up(mid[1], zero if hi_parts is None else hi_parts[1])
+
+    def bands(outer_tile, edge_tile, inner_tile):
+        south_edge = outer_tile < edge_tile
+        main_coefs(outer_tile)
+        main_coefs(edge_tile)
+        for k in range(ITERS):
+            def band(g, carry):
+                far, mid, near = (
+                    member_parts(k, g, t) for t in (outer_tile, edge_tile, inner_tile))
+                ordered = (far[1], mid[1], near[1]) if south_edge else (near[1], mid[1], far[1])
+                if k + 1 < ITERS:
+                    vk[k, g, at(outer_tile), :] = (
+                        join(None, far[1], mid[1]) if south_edge else join(mid[1], far[1], None))
+                out = join(*ordered)
+                vk[k, g, at(edge_tile), :] = out
+                x = mid[0]
+                w = cen[at(edge_tile - first), :] * x
+                macc[2 * k, g] = macc[2 * k, g] + w * x
+                macc[2 * k + 1, g] = macc[2 * k + 1, g] + w * out
+                return carry
+            lax.fori_loop(0, members, band, 0, unroll=members)
+
+    def take_rows(side, tile, seen):
+        rs = at(tile)
+
+        def clean(x):
+            return jnp.where(seen, x, 0.0)
+        for a in range(ARRAYS):
+            if a not in (RIM, KRIM):
+                st[a, rs, :] = clean(rowin[side, a])
+
+    def take_corners(side, tile, seen):
+        def clean(x):
+            return jnp.where(seen, x, 0.0)
+        o, k = clean(rowin[side, RIM]), clean(rowin[side, KRIM])
+        ow, kw = (clean(diagin[2 * side, i]) for i in range(2))
+        oe, ke = (roll(clean(diagin[2 * side + 1, i]), 10) for i in range(2))
+        put_strip(at(tile), unfold(o, k, ow, kw, oe, ke))
+
+    @pl.when(not_first)
+    def _():
+        up[0].wait_recv()
+        take_rows(0, first - 1, sub > 4)
+
+    @pl.when(lat_first)
+    def _():
+        rs = at(first - 1)
+        for a in range(ARRAYS):
+            st[a, rs, :] = zero
+        put_strip(rs, (zero, zero, zero))
+
+    bands(first - 1, first, first + 1)
+
+    @pl.when(not_last)
+    def _():
+        down[0].wait_recv()
+        take_rows(1, last + 1, sub < 3)
+        bands(last + 1, last, last - 1)
+
     for c in sides:
         c.wait_recv()
 
@@ -324,41 +463,26 @@
         return carry
     lax.fori_loop(0, tiles // 4, merge, 0, unroll=split(tiles // 4, 6))
 
-    def take_rows(side, tile, seen):
-        rs = at(tile)
-
-        def clean(x):
-            return jnp.where(seen, x, 0.0)
-        for a in range(ARRAYS):
-            if a not in (RIM, KRIM):
-                st[a, rs, :] = clean(rowin[side, a])
-        o, k = clean(rowin[side, RIM]), clean(rowin[side, KRIM])
-        ow, kw = (clean(diagin[2 * side, i]) for i in range(2))
-        oe, ke = (roll(clean(diagin[2 * side + 1, i]), 10) for i in range(2))
-        put_strip(rs, unfold(o, k, ow, kw, oe, ke))
-
     @pl.when(not_first)
     def _():
-        for c in up:
+        for c in up[1:]:
             c.wait_recv()
-        take_rows(0, first - 1, sub > 4)
-
-    @pl.when(lat_first)
-    def _():
-        rs = at(first - 1)
-        for a in range(ARRAYS):
-            st[a, rs, :] = zero
-        put_strip(rs, (zero, zero, zero))
+        take_corners(0, first - 1, sub > 4)
 
     @pl.when(not_last)
     def _():
-        for c in down:
+        for c in down[1:]:
             c.wait_recv()
-        take_rows(1, last + 1, sub < 3)
+        take_corners(1, last + 1, sub < 3)
+
+    def edge_spread(t, carry):
+        spread_tile(first - 1 + t)
+        return carry
+    lax.fori_loop(0, tiles, edge_spread, 0, unroll=split(tiles, 24))
 
     @pl.when(lat_last)
     def _():
-        for c in folds:
+        for c in folds[:1] + relays:
             c.wait_recv()
         total = lon_count * cols
         rs = at(last + 1)
@@ -369,7 +493,7 @@
             start = lax.rem(origin + shift + total, total)
             chunk = lax.div(start, cols)
             head = start - chunk * cols
-            slots = [lax.rem(lo - chunk - o + 3 * lon_count, lon_count) for o in (1, 0, -1, -2)]
+            slots = [lax.rem(chunk + o + 2 * lon_count, lon_count) for o in (1, 0, -1, -2)]
             z = head - shown
             return (slots, jnp.bitwise_and(head - lane, cols - 1), lane <= head,
                     jnp.bitwise_and(z, cols - 1), (z >= cols, z >= 0, z >= -cols))
@@ -382,7 +506,7 @@
         blocks = []
         for i, a in enumerate(fold_arrays):
             slots, where, within, where_s, (far, near, back) = views[shifts.get(a, 0)]
-            chunks = [jnp.where(sub < 3, fold[s, i], 0.0) for s in slots]
+            chunks = [jnp.where(sub < len(fold_picks[a]), fold[s, pl.ds(fold_start[i], 8), :], 0.0) for s in slots]
             block = jnp.where(within, take(chunks[1], where), take(chunks[2], where))
             st[a, rs, :] = block
             blocks.append(block)
@@ -394,30 +518,27 @@
             if a == NORTH:
                 end = pl.ds(EDGE + rows - 1, 1)
                 st[NORTH, end, :] = 0.5 * (st[NORTH, end, :] + block[2:3, :])
-                mixed = 0.5 * (kstrip[end, :] + x[2:3, :])
-                g1, l1 = group[0:1, :], lane[0:1, :]
-                dropped = jnp.logical_or(jnp.logical_or(g1 == 2, g1 == 3),
-                                         jnp.logical_or(l1 == EXTRA + 1, l1 == EXTRA + 2))
-                kstrip[end, :] = jnp.where(
-                    dropped, 0.0, jnp.where(g1 == 1, mixed, kstrip[end, :]))
+                red[0] = x
                 st[NEAST, end, :] = jnp.zeros((1, cols), f32)
                 st[NWEST, end, :] = jnp.zeros((1, cols), f32)
         o, k = rim(blocks[:members]), rim(blocks[members:])
         ring = unfold(o, k, zero, zero, zero, zero)[1]
         put_strip(rs, (ghost[0], ring, extras(ghost[1], k)))
-
-    for tile in (first - 1, first, last, last + 1):
-        main_coefs(tile)
+        end = pl.ds(EDGE + rows - 1, 1)
+        mixed = 0.5 * (kstrip[end, :] + red[0, pl.ds(2, 1), :])
+        g1, l1 = group[0:1, :], lane[0:1, :]
+        dropped = jnp.logical_or(jnp.logical_or(g1 == 2, g1 == 3),
+                                 jnp.logical_or(l1 == EXTRA + 1, l1 == EXTRA + 2))
+        kstrip[end, :] = jnp.where(dropped, 0.0, jnp.where(g1 == 1, mixed, kstrip[end, :]))
+        bands(last + 1, last, last - 1)
+
+    spread_tile(last)
+    spread_tile(last + 1)
 
     def edge_coefs(t, carry):
         strip_coefs(first - 1 + t)
         return carry
     lax.fori_loop(0, tiles + 2, edge_coefs, 0, unroll=split(tiles + 2, 26))
-
-    def join(lo_parts, mid, hi_parts):
-        out = mid[0]
-        out = out + shift_down(zero if lo_parts is None else lo_parts[2], mid[2])
-        return out + shift_up(mid[1], zero if hi_parts is None else hi_parts[1])
 
     for k in range(ITERS):
         _, (cross, upper, lower) = strip_parts(k, first - 1)
@@ -443,25 +564,6 @@
         sacc[2 * k] = acc0
         sacc[2 * k + 1] = acc1 + w_old * out
 
-        def band(g, carry):
-            b = [member_parts(k, g, t) for t in (first - 1, first, first + 1)]
-            t = [member_parts(k, g, t) for t in (last - 1, last, last + 1)]
-            if k + 1 < ITERS:
-                vk[k, g, at(first - 1), :] = join(None, b[0][1], b[1][1])
-                vk[k, g, at(last + 1), :] = join(t[1][1], t[2][1], None)
-            acc0, acc1 = macc[2 * k, g], macc[2 * k + 1, g]
-            for tile, three in ((first, b), (last, t)):
-                out = join(three[0][1], three[1][1], three[2][1])
-                vk[k, g, at(tile), :] = out
-                x = three[1][0]
-                w = cen[at(tile - first), :] * x
-                acc0 = acc0 + w * x
-                acc1 = acc1 + w * out
-            macc[2 * k, g] = acc0
-            macc[2 * k + 1, g] = acc1
-            return carry
-        lax.fori_loop(0, members, band, 0, unroll=members)
-
     def column_sum(x):
         for s in (4, 2, 1):
             x = x + roll(x, s, 0)
@@ -500,8 +602,8 @@
 
     outer = jnp.logical_or(lane < 3, lane > cols - 4)
 
-    def close_rims():
-        for k in range(1, ITERS + 1):
+    def close_rims(stages):
+        for k in stages:
             def close(t, carry):
                 rs = at(first + t)
                 x = strips[k, rs, :]
@@ -513,9 +615,9 @@
             lax.fori_loop(0, tiles, close, 0, unroll=split(tiles, 8))
 
     row, c1 = reduce(row, 0, redlon, lo, lon_ss, lon_rs, lon_count,
-                     lambda d: (la, lax.rem(lo + d, lon_count)), close_rims)
+                     lambda d: (la, lax.rem(lo + d, lon_count)), lambda: close_rims((1, 2)))
     row, c2 = reduce(row, 1, redlat, la, lat_ss, lat_rs, lat_count,
-                     lambda d: (lax.rem(la + d, lat_count), lo))
+                     lambda d: (lax.rem(la + d, lat_count), lo), lambda: close_rims((3,)))
 
     m0, m1, m2, m3, m4, m5 = (
         jnp.broadcast_to(
@@ -553,7 +655,7 @@
 
     @pl.when(lat_last)
     def _():
-        for c in folds:
+        for c in folds + relays:
             c.wait_send()
 
 
@@ -586,7 +688,7 @@
     shape = jax.ShapeDtypeStruct(right_side.shape, f32)
     high = rows + 2 * EDGE
     tiles = rows // 8
-    folded = members + len(COUPLED)
+    folded = -(-3 * (members + len(COUPLED)) // 8) * 8 + 8
     st, vk, mix, cen = pl.pallas_call(
         functools.partial(kernel, lat_count, lon_count),
         out_shape=(pltpu.VMEM((ARRAYS, high, cols), f32),
@@ -603,17 +705,18 @@
             pltpu.VMEM((high, cols), f32),
             pltpu.VMEM((8, high, cols), f32),
             pltpu.VMEM((9, high, cols), f32),
+            pltpu.VMEM((4, high, cols), f32),
             pltpu.VMEM((2, 2, tiles // 4, 8, cols), f32),
             pltpu.VMEM((2, 2, tiles // 4, 8, cols), f32),
             pltpu.VMEM((2, ARRAYS, 8, cols), f32),
             pltpu.VMEM((4, 2, 8, cols), f32),
-            pltpu.VMEM((lon_count, folded, 8, cols), f32),
+            pltpu.VMEM((lon_count, folded, cols), f32),
             pltpu.VMEM((2 * ITERS, members, 8, cols), f32),
             pltpu.VMEM((2 * ITERS, 8, cols), f32),
             pltpu.VMEM((2, 8, cols), f32),
             pltpu.VMEM((lon_count, 8, cols), f32),
             pltpu.VMEM((lat_count, 8, cols), f32),
-            dma((5,)), dma((8,)), dma((8,)),
+            dma((3, 5)), dma((8,)), dma((8,)),
             dma((lon_count,)), dma((lon_count,)),
             dma((lon_count,)), dma((lon_count,)),
             dma((lat_count,)), dma((lat_count,)),

time: 23.6 us -> 21.9 us (0.928)
  Pallas kernels: 22.8 us -> 21.1 us
    pallas_call x1, Pallas kernels: 21.5 us -> 19.7 us  [body(): pl.pallas_call(functools.partial(kernel, lat_count, lon_count), out_shape...]
where the time goes in v3:
time: 21.9 us; the launch traced here: 21.7 us
  Pallas kernels  21.1 us (96%)
  between operations  0.64 us (3%)
    pallas_call x1, Pallas kernels, body(): pl.pallas_call(functools.partial(kernel, lat_count, lon_count), out_shape...  19.7 us
    pallas_call x1, Pallas kernels, body(): pl.pallas_call(finish, out_shape=(shape, shape), in_specs=[vmem] * 4, out...  1.31 us

profile of v3, /device:TPU:0, one launch (start us, length us, event | category | flops | bytes accessed | tf_op | source)
XLA Modules:
  0.0 21.7 jit_solution(6103836070746721619)
XLA Ops:
  0.6 19.7 %shard_map.68 = (f32[15,224,128]{2,1,0:T(8,128)S(1)}, f32[3,8,224,128]{3,2,1,0:T(8,128)S(1)}, f32[7,8,128]{2,1,0:T(8,128)S(1)}, f32[192,128]{1,0:T(8,128)S(1)}) custom-call(f32[8,192,128]{2,1,0:T(8,128)} %rhs.1, f32[192,128]{1,0:T(8,128)} %center_hbm.1, f32[4,192,128]{2,1,0:T(8,128)} %coup_hbm.1, s32[192,128]{1,0:T(8,128)} %land_hbm.1, s32[8,128]{1,0:T(8,128)} %bitcast.1), custom_call_target="tpu_custom_call" | custom-call | tf_op jit(solution)/shard_map/pallas_call | solution.py:692
  20.4 1.3 %shard_map.69 = (f32[8,192,128]{2,1,0:T(8,128)}, f32[8,192,128]{2,1,0:T(8,128)}) custom-call(f32[15,224,128]{2,1,0:T(8,128)S(1)} %get-tuple-element.6.st, f32[3,8,224,128]{3,2,1,0:T(8,128)S(1)} %get-tuple-element.7.vk, f32[7,8,128]{2,1,0:T(8,128)S(1)} %get-tuple-element.8.mix, f32[192,128]{1,0:T(8,128)S(1)} %get-tuple-element.9.center), custom_call_target="tpu_custom_call" | custom-call | tf_op jit(solution)/shard_map/pallas_call | solution.py:728

commit v4 on v3

--- a/solution.py
+++ b/solution.py
@@ -15,7 +15,7 @@
 RIM, KRIM, EAST, NORTH, NEAST, NWEST, SCALE, ARRAYS = range(8, 16)
 EXTRA = 5 * SLOT
 COUPLED = (EAST, NORTH, NEAST, NWEST, SCALE)
-FROM_S, FROM_N, FROM_SW, FROM_SE, FROM_NW, FROM_NE, FROM_W, FROM_E = range(8)
+SIDES, UP, DOWN, UP_CORNERS, DOWN_CORNERS = range(5)
 
 
 def roll(x, shift, axis=1):
@@ -27,7 +27,7 @@
     rhs, center_hbm, coup_hbm, land_hbm, partner_hbm, st, vk, mix, cen,
     land, partner, strips, kstrip, beyond, coefm, coefs, wide, pack, packin, rowin, diagin, fold,
     macc, sacc, red, redlon, redlat,
-    load_sem, send_sem, recv_sem, fold_ss, fold_rs, lon_ss, lon_rs, lat_ss, lat_rs,
+    load_sem, send_sem, recv_sem, fold_sem, red_sem,
 ):
     f32 = jnp.float32
     members, rows, cols = rhs.shape
@@ -57,14 +57,14 @@
     for i, (start, size) in enumerate(((0, 8), (rows - 8, 8), (8, rows - 16))):
         rs, own = pl.ds(start, size), pl.ds(EDGE + start, size)
         loads += [
-            pltpu.make_async_copy(center_hbm.at[rs], cen.at[rs], load_sem.at[i, 0]),
-            pltpu.make_async_copy(land_hbm.at[rs], land.at[rs], load_sem.at[i, 1]),
+            pltpu.make_async_copy(center_hbm.at[rs], cen.at[rs], load_sem.at[i // 2]),
+            pltpu.make_async_copy(land_hbm.at[rs], land.at[rs], load_sem.at[i // 2]),
             pltpu.make_async_copy(coup_hbm.at[:, rs], st.at[pl.ds(EAST, 4), own],
-                                  load_sem.at[i, 2]),
+                                  load_sem.at[i // 2]),
             pltpu.make_async_copy(rhs.at[:, rs], st.at[pl.ds(0, members), own],
-                                  load_sem.at[i, 3]),
+                                  load_sem.at[i // 2]),
         ]
-    loads.append(pltpu.make_async_copy(partner_hbm.at[pl.ds(0, 1)], partner, load_sem.at[0, 4]))
+    loads.append(pltpu.make_async_copy(partner_hbm.at[pl.ds(0, 1)], partner, load_sem.at[2]))
     for c in loads:
         c.start()
 
@@ -128,21 +128,21 @@
 
     top, bottom = pl.ds(EDGE + rows - 3, 3), pl.ds(EDGE, 3)
 
-    def remote(src, dst, slot, dev):
+    def remote(src, dst, slot, landing, dev):
         return pltpu.make_async_remote_copy(
-            src_ref=src, dst_ref=dst, send_sem=send_sem.at[slot], recv_sem=recv_sem.at[slot],
+            src_ref=src, dst_ref=dst, send_sem=send_sem.at[slot], recv_sem=recv_sem.at[landing],
             device_id=dev, device_id_type=MESH)
 
-    sides = [remote(pack.at[0], packin.at[0], FROM_W, (la, east)),
-             remote(pack.at[1], packin.at[1], FROM_E, (la, west))]
+    sides = [remote(pack.at[0], packin.at[0], SIDES, SIDES, (la, east)),
+             remote(pack.at[1], packin.at[1], SIDES, SIDES, (la, west))]
     pair = pl.ds(RIM, 2)
     low, high = pl.ds(5, 3), pl.ds(0, 3)
-    up = [remote(st.at[:, top], rowin.at[0, :, low], FROM_S, (north, lo)),
-          remote(st.at[pair, top], diagin.at[0, :, low], FROM_SW, (north, east)),
-          remote(st.at[pair, top], diagin.at[1, :, low], FROM_SE, (north, west))]
-    down = [remote(st.at[:, bottom], rowin.at[1, :, high], FROM_N, (south, lo)),
-            remote(st.at[pair, bottom], diagin.at[2, :, high], FROM_NW, (south, east)),
-            remote(st.at[pair, bottom], diagin.at[3, :, high], FROM_NE, (south, west))]
+    up = [remote(st.at[:, top], rowin.at[0, :, low], UP, UP, (north, lo)),
+          remote(st.at[pair, top], diagin.at[0, :, low], UP, UP_CORNERS, (north, east)),
+          remote(st.at[pair, top], diagin.at[1, :, low], UP, UP_CORNERS, (north, west))]
+    down = [remote(st.at[:, bottom], rowin.at[1, :, high], DOWN, DOWN, (south, lo)),
+            remote(st.at[pair, bottom], diagin.at[2, :, high], DOWN, DOWN_CORNERS, (south, east)),
+            remote(st.at[pair, bottom], diagin.at[3, :, high], DOWN, DOWN_CORNERS, (south, west))]
     fold_arrays = list(range(members)) + list(COUPLED)
     fold_picks = {a: (0, 1, 2) for a in range(members)}
     fold_picks.update({EAST: (0, 1), NORTH: (1, 2, 0), NEAST: (1, 2), NWEST: (1, 2), SCALE: (0, 1)})
@@ -153,18 +153,21 @@
     mate = lo + 1 - 2 * lax.rem(lo, 2)
     half = lon_count // 2
 
-    def fold_copy(sender, slot, dev):
+    def fold_copy(sender, landing, dev):
         return pltpu.make_async_remote_copy(
             src_ref=fold.at[sender, sent], dst_ref=fold.at[sender, sent],
-            send_sem=fold_ss.at[slot], recv_sem=fold_rs.at[slot],
+            send_sem=fold_sem.at[0], recv_sem=fold_sem.at[landing],
             device_id=(la, dev), device_id_type=MESH)
-    folds = [fold_copy(lo, 0, mate)]
-    folds += [fold_copy(lo, j, lax.rem(lo + 2 * j, lon_count)) for j in range(1, half)]
-    relays = [fold_copy(lax.rem(lo + lon_count - 2 * j, lon_count), half + j, mate)
+    folds = [fold_copy(lo, 2, mate)]
+    folds += [fold_copy(lo, 1, lax.rem(lo + 2 * j, lon_count)) for j in range(1, half)]
+    relays = [fold_copy(lax.rem(lo + lon_count - 2 * j, lon_count), 2, mate)
               for j in range(1, half)]
 
-    for c in loads[:8]:
-        c.wait()
+    def settle(ref, sem):
+        pltpu.make_async_copy(ref, ref, sem).wait()
+
+    blocks = members + 6
+    settle(st.at[pl.ds(0, blocks), pl.ds(0, 16)], load_sem.at[0])
     prep_tile(first)
     prep_tile(last)
 
@@ -192,8 +195,8 @@
         pl.semaphore_wait(barrier, arrivals)
         send_folds()
 
-    for c in loads[8:]:
-        c.wait()
+    settle(st.at[pl.ds(0, blocks), pl.ds(0, rows - 16)], load_sem.at[1])
+    loads[-1].wait()
     lax.fori_loop(0, inner, prep, 0, unroll=split(inner, 11))
     lax.fori_loop(0, tiles // 4, fill, 0, unroll=split(tiles // 4, 6))
 
@@ -378,8 +381,7 @@
 
     @pl.when(lat_last)
     def _():
-        for c in folds[1:]:
-            c.wait_recv()
+        settle(fold.at[pl.ds(0, half - 1), sent], fold_sem.at[1])
         for c in relays:
             c.start()
 
@@ -428,7 +430,7 @@
 
     @pl.when(not_first)
     def _():
-        up[0].wait_recv()
+        settle(rowin.at[0, :, low], recv_sem.at[UP])
         take_rows(0, first - 1, sub > 4)
 
     @pl.when(lat_first)
@@ -442,12 +444,11 @@
 
     @pl.when(not_last)
     def _():
-        down[0].wait_recv()
+        settle(rowin.at[1, :, high], recv_sem.at[DOWN])
         take_rows(1, last + 1, sub < 3)
         bands(last + 1, last, last - 1)
 
-    for c in sides:
-        c.wait_recv()
+    settle(packin, recv_sem.at[SIDES])
 
     def merge(t, carry):
         fw, fe = [packin[0, g, t] for g in range(2)], [packin[1, g, t] for g in range(2)]
@@ -463,27 +464,24 @@
         return carry
     lax.fori_loop(0, tiles // 4, merge, 0, unroll=split(tiles // 4, 6))
 
+    def edge_spread(t, carry):
+        spread_tile(first + t)
+        return carry
+    lax.fori_loop(0, tiles - 1, edge_spread, 0, unroll=split(tiles - 1, 23))
+
     @pl.when(not_first)
     def _():
-        for c in up[1:]:
-            c.wait_recv()
+        settle(diagin.at[pl.ds(0, 2), :, low], recv_sem.at[UP_CORNERS])
         take_corners(0, first - 1, sub > 4)
 
     @pl.when(not_last)
     def _():
-        for c in down[1:]:
-            c.wait_recv()
+        settle(diagin.at[pl.ds(2, 2), :, high], recv_sem.at[DOWN_CORNERS])
         take_corners(1, last + 1, sub < 3)
 
-    def edge_spread(t, carry):
-        spread_tile(first - 1 + t)
-        return carry
-    lax.fori_loop(0, tiles, edge_spread, 0, unroll=split(tiles, 24))
-
     @pl.when(lat_last)
     def _():
-        for c in folds[:1] + relays:
-            c.wait_recv()
+        settle(fold.at[pl.ds(0, half), sent], fold_sem.at[2])
         total = lon_count * cols
         rs = at(last + 1)
         shown = jnp.where(place < 8, place - 3, place + (cols - 13))
@@ -532,6 +530,7 @@
         kstrip[end, :] = jnp.where(dropped, 0.0, jnp.where(g1 == 1, mixed, kstrip[end, :]))
         bands(last + 1, last, last - 1)
 
+    spread_tile(first - 1)
     spread_tile(last)
     spread_tile(last + 1)
 
@@ -580,25 +579,25 @@
 
     row = column_sum(row)
 
-    def reduce(value, slot, recv, me, ss, rs, count, dev, between=None):
+    def reduce(value, slot, recv, me, count, dev, between):
         red[slot] = value
+        mine = pl.ds(me, 1)
         cps = [
             pltpu.make_async_remote_copy(
-                src_ref=red.at[slot, pl.ds(0, 1)], dst_ref=recv.at[me, pl.ds(0, 1)],
-                send_sem=ss.at[d], recv_sem=rs.at[d], device_id=dev(d), device_id_type=MESH)
+                src_ref=red.at[slot, pl.ds(0, 1)], dst_ref=recv.at[mine],
+                send_sem=red_sem.at[2 * slot], recv_sem=red_sem.at[2 * slot + 1],
+                device_id=dev(d), device_id_type=MESH)
             for d in range(1, count)
         ]
         for c in cps:
             c.start()
-        recv[me] = value
-        if between:
-            between()
-        for c in cps:
-            c.wait_recv()
-        out = recv[0, pl.ds(0, 1), :]
+        recv[mine, :] = value[0:1, :]
+        between()
+        settle(recv.at[pl.ds(0, count - 1)], red_sem.at[2 * slot + 1])
+        out = recv[pl.ds(0, 1), :]
         for d in range(1, count):
-            out = out + recv[d, pl.ds(0, 1), :]
-        return jnp.broadcast_to(out, (8, cols)), cps
+            out = out + recv[pl.ds(d, 1), :]
+        return jnp.broadcast_to(out, (8, cols))
 
     outer = jnp.logical_or(lane < 3, lane > cols - 4)
 
@@ -614,10 +613,10 @@
                 return carry
             lax.fori_loop(0, tiles, close, 0, unroll=split(tiles, 8))
 
-    row, c1 = reduce(row, 0, redlon, lo, lon_ss, lon_rs, lon_count,
-                     lambda d: (la, lax.rem(lo + d, lon_count)), lambda: close_rims((1, 2)))
-    row, c2 = reduce(row, 1, redlat, la, lat_ss, lat_rs, lat_count,
-                     lambda d: (lax.rem(la + d, lat_count), lo), lambda: close_rims((3,)))
+    row = reduce(row, 0, redlon, lo, lon_count,
+                 lambda d: (la, lax.rem(lo + d, lon_count)), lambda: close_rims((1, 2)))
+    row = reduce(row, 1, redlat, la, lat_count,
+                 lambda d: (lax.rem(la + d, lat_count), lo), lambda: close_rims((3,)))
 
     m0, m1, m2, m3, m4, m5 = (
         jnp.broadcast_to(
@@ -640,23 +639,21 @@
     for i, value in enumerate((q3 + q2 + q1, q2 + q3, q3, q0, q1, q2, q3)):
         mix[i] = value
 
-    for c in sides + c1 + c2:
-        c.wait_send()
+    settle(pack, send_sem.at[SIDES])
+    settle(redlon.at[pl.ds(0, lon_count - 1)], red_sem.at[0])
+    settle(redlat.at[pl.ds(0, lat_count - 1)], red_sem.at[2])
 
     @pl.when(not_last)
     def _():
-        for c in up:
-            c.wait_send()
+        settle(st.at[0, pl.ds(0, 3 * (ARRAYS + 4))], send_sem.at[UP])
 
     @pl.when(not_first)
     def _():
-        for c in down:
-            c.wait_send()
+        settle(st.at[0, pl.ds(0, 3 * (ARRAYS + 4))], send_sem.at[DOWN])
 
     @pl.when(lat_last)
     def _():
-        for c in folds + relays:
-            c.wait_send()
+        settle(fold.at[pl.ds(0, 2 * half - 1), sent], fold_sem.at[0])
 
 
 def finish(st, vk, mix, center, sol_out, res_out, obuf, store_sem):
@@ -671,12 +668,10 @@
             obuf[0, m, here, :] = s0 * v0 + s1 * v1 + s2 * v2
             obuf[1, m, here, :] = center[here, :] * (q0 * v0 + q1 * v1 + q2 * v2 + q3 * v3)
         for o, dst in ((0, sol_out), (1, res_out)):
-            pltpu.make_async_copy(obuf.at[o, m], dst.at[m], store_sem.at[o, m]).start()
+            pltpu.make_async_copy(obuf.at[o, m], dst.at[m], store_sem.at[0]).start()
         return carry
     lax.fori_loop(0, members, one, 0)
-    for m in range(members):
-        for o, dst in ((0, sol_out), (1, res_out)):
-            pltpu.make_async_copy(obuf.at[o, m], dst.at[m], store_sem.at[o, m]).wait()
+    pltpu.make_async_copy(obuf, obuf, store_sem.at[0]).wait()
 
 
 def body(lat_count, lon_count, right_side, center, couplings, land_sea, fold_partner):
@@ -714,12 +709,9 @@
             pltpu.VMEM((2 * ITERS, members, 8, cols), f32),
             pltpu.VMEM((2 * ITERS, 8, cols), f32),
             pltpu.VMEM((2, 8, cols), f32),
-            pltpu.VMEM((lon_count, 8, cols), f32),
-            pltpu.VMEM((lat_count, 8, cols), f32),
-            dma((3, 5)), dma((8,)), dma((8,)),
-            dma((lon_count,)), dma((lon_count,)),
-            dma((lon_count,)), dma((lon_count,)),
-            dma((lat_count,)), dma((lat_count,)),
+            pltpu.VMEM((-(-lon_count // 8) * 8, cols), f32),
+            pltpu.VMEM((-(-lat_count // 8) * 8, cols), f32),
+            dma((3,)), dma((3,)), dma((5,)), dma((3,)), dma((4,)),
         ],
         compiler_params=pltpu.CompilerParams(
             collective_id=0, has_side_effects=True, vmem_limit_bytes=32 * 1024 * 1024),
@@ -732,7 +724,7 @@
         out_specs=(hbm, hbm),
         scratch_shapes=[
             pltpu.VMEM((2, members, rows, cols), f32),
-            dma((2, members)),
+            dma((1,)),
         ],
         compiler_params=pltpu.CompilerParams(vmem_limit_bytes=16 * 1024 * 1024),
     )(st, vk, mix, cen)

time: 21.9 us -> 21.1 us (0.963)
  Pallas kernels: 21.1 us -> 20.3 us
    pallas_call x1, Pallas kernels: 19.7 us -> 19.2 us  [body(): pl.pallas_call(functools.partial(kernel, lat_count, lon_count), out_shape...]
where the time goes in v4:
time: 21.1 us; the launch traced here: 21 us
  Pallas kernels  20.3 us (96%)
  between operations  0.64 us (3%)
    pallas_call x1, Pallas kernels, body(): pl.pallas_call(functools.partial(kernel, lat_count, lon_count), out_shape...  19.2 us
    pallas_call x1, Pallas kernels, body(): pl.pallas_call(finish, out_shape=(shape, shape), in_specs=[vmem] * 4, out...  1.18 us

profile of v4, /device:TPU:0, one launch (start us, length us, event | category | flops | bytes accessed | tf_op | source)
XLA Modules:
  0.0 21.0 jit_solution(6510717002541075768)
XLA Ops:
  0.6 19.2 %shard_map.68 = (f32[15,224,128]{2,1,0:T(8,128)S(1)}, f32[3,8,224,128]{3,2,1,0:T(8,128)S(1)}, f32[7,8,128]{2,1,0:T(8,128)S(1)}, f32[192,128]{1,0:T(8,128)S(1)}) custom-call(f32[8,192,128]{2,1,0:T(8,128)} %rhs.1, f32[192,128]{1,0:T(8,128)} %center_hbm.1, f32[4,192,128]{2,1,0:T(8,128)} %coup_hbm.1, s32[192,128]{1,0:T(8,128)} %land_hbm.1, s32[8,128]{1,0:T(8,128)} %bitcast.1), custom_call_target="tpu_custom_call" | custom-call | tf_op jit(solution)/shard_map/pallas_call | solution.py:687
  19.8 1.2 %shard_map.69 = (f32[8,192,128]{2,1,0:T(8,128)}, f32[8,192,128]{2,1,0:T(8,128)}) custom-call(f32[15,224,128]{2,1,0:T(8,128)S(1)} %get-tuple-element.6.st, f32[3,8,224,128]{3,2,1,0:T(8,128)S(1)} %get-tuple-element.7.vk, f32[7,8,128]{2,1,0:T(8,128)S(1)} %get-tuple-element.8.mix, f32[192,128]{1,0:T(8,128)S(1)} %get-tuple-element.9.center), custom_call_target="tpu_custom_call" | custom-call | tf_op jit(solution)/shard_map/pallas_call | solution.py:720

commit v5 on v4

--- a/solution.py
+++ b/solution.py
@@ -15,7 +15,7 @@
 RIM, KRIM, EAST, NORTH, NEAST, NWEST, SCALE, ARRAYS = range(8, 16)
 EXTRA = 5 * SLOT
 COUPLED = (EAST, NORTH, NEAST, NWEST, SCALE)
-SIDES, UP, DOWN, UP_CORNERS, DOWN_CORNERS = range(5)
+SIDES, UP, DOWN, UP_CORNERS, DOWN_CORNERS, SIDES_K = range(6)
 
 
 def roll(x, shift, axis=1):
@@ -26,8 +26,8 @@
     lat_count, lon_count,
     rhs, center_hbm, coup_hbm, land_hbm, partner_hbm, st, vk, mix, cen,
     land, partner, strips, kstrip, beyond, coefm, coefs, wide, pack, packin, rowin, diagin, fold,
-    macc, sacc, red, redlon, redlat,
-    load_sem, send_sem, recv_sem, fold_sem, red_sem,
+    macc, sacc, red, spare, redin,
+    load_sem, send_sem, recv_sem, fold_sem, red_sem, known,
 ):
     f32 = jnp.float32
     members, rows, cols = rhs.shape
@@ -65,9 +65,8 @@
                                   load_sem.at[i // 2]),
         ]
     loads.append(pltpu.make_async_copy(partner_hbm.at[pl.ds(0, 1)], partner, load_sem.at[2]))
-    for c in loads:
+    for c in loads[:8]:
         c.start()
-
     barrier = pltpu.get_barrier_semaphore()
     partners = [(la, lax.rem(lo + d, lon_count)) for d in range(1, lon_count)]
     partners += [(lax.rem(la + d, lat_count), lo) for d in range(1, lat_count)]
@@ -84,6 +83,8 @@
         for p in ((south, east), (south, west)):
             pl.semaphore_signal(barrier, inc=1, device_id=p, device_id_type=MESH)
     arrivals = (len(partners) + 2 * jnp.where(not_last, 1, 0) + 2 * jnp.where(not_first, 1, 0))
+    for c in loads[8:]:
+        c.start()
 
     rim_lanes = [jnp.bitwise_and(lane - (SLOT * g - 3), cols - 1) < 12 for g in range(8)]
 
@@ -133,8 +134,10 @@
             src_ref=src, dst_ref=dst, send_sem=send_sem.at[slot], recv_sem=recv_sem.at[landing],
             device_id=dev, device_id_type=MESH)
 
-    sides = [remote(pack.at[0], packin.at[0], SIDES, SIDES, (la, east)),
-             remote(pack.at[1], packin.at[1], SIDES, SIDES, (la, west))]
+    def side_copies(g, landing):
+        return [remote(pack.at[0, g], packin.at[0, g], SIDES, landing, (la, east)),
+                remote(pack.at[1, g], packin.at[1, g], SIDES, landing, (la, west))]
+    sides, sides_k = side_copies(0, SIDES), side_copies(1, SIDES_K)
     pair = pl.ds(RIM, 2)
     low, high = pl.ds(5, 3), pl.ds(0, 3)
     up = [remote(st.at[:, top], rowin.at[0, :, low], UP, UP, (north, lo)),
@@ -211,17 +214,14 @@
         if lat_count > 1:
             for c in down:
                 c.start()
-        for c in folds[:half // 2:-1]:
+        for c in folds[::-1]:
             c.start()
 
-    sides[1].start()
-
-    @pl.when(send_later)
-    def _():
-        for c in folds[:1] + folds[half // 2:0:-1]:
-            c.start()
-
-    sides[0].start()
+    for c in (sides_k[1], sides[1], sides_k[0], sides[0]):
+        c.start()
+    for d in range(1, lat_count):
+        pl.semaphore_signal(known, inc=1, device_id=(lax.rem(la + d, lat_count), lo),
+                            device_id_type=MESH)
 
     @pl.when(not_last)
     def _():
@@ -448,26 +448,28 @@
         take_rows(1, last + 1, sub < 3)
         bands(last + 1, last, last - 1)
 
-    settle(packin, recv_sem.at[SIDES])
-
-    def merge(t, carry):
-        fw, fe = [packin[0, g, t] for g in range(2)], [packin[1, g, t] for g in range(2)]
-        for q in range(4):
-            rs = at(first + t * 4 + q)
-            for g, ref in enumerate((strips.at[0], kstrip)):
+    def merge(g, ref):
+        def step(t, carry):
+            fw, fe = packin[0, g, t], packin[1, g, t]
+            for q in range(4):
+                rs = at(first + t * 4 + q)
                 x = ref[rs, :]
                 keep = lane < EXTRA if g else lane >= 0
                 x = jnp.where(jnp.logical_and(place < 3, keep),
-                              roll(fw[g], (-3 * q) % cols) if q else fw[g], x)
-                x = jnp.where(jnp.logical_and(place > 12, keep), roll(fe[g], 10 - 3 * q), x)
-                ref[rs, :] = x
-        return carry
-    lax.fori_loop(0, tiles // 4, merge, 0, unroll=split(tiles // 4, 6))
+                              roll(fw, (-3 * q) % cols) if q else fw, x)
+                ref[rs, :] = jnp.where(jnp.logical_and(place > 12, keep), roll(fe, 10 - 3 * q), x)
+            return carry
+        lax.fori_loop(0, tiles // 4, step, 0, unroll=split(tiles // 4, 6))
+    settle(packin.at[:, 1], recv_sem.at[SIDES_K])
+    merge(1, kstrip)
 
     def edge_spread(t, carry):
         spread_tile(first + t)
         return carry
     lax.fori_loop(0, tiles - 1, edge_spread, 0, unroll=split(tiles - 1, 23))
+
+    settle(packin.at[:, 0], recv_sem.at[SIDES])
+    merge(0, strips.at[0])
 
     @pl.when(not_first)
     def _():
@@ -516,14 +518,14 @@
             if a == NORTH:
                 end = pl.ds(EDGE + rows - 1, 1)
                 st[NORTH, end, :] = 0.5 * (st[NORTH, end, :] + block[2:3, :])
-                red[0] = x
+                spare[...] = x
                 st[NEAST, end, :] = jnp.zeros((1, cols), f32)
                 st[NWEST, end, :] = jnp.zeros((1, cols), f32)
         o, k = rim(blocks[:members]), rim(blocks[members:])
         ring = unfold(o, k, zero, zero, zero, zero)[1]
         put_strip(rs, (ghost[0], ring, extras(ghost[1], k)))
         end = pl.ds(EDGE + rows - 1, 1)
-        mixed = 0.5 * (kstrip[end, :] + red[0, pl.ds(2, 1), :])
+        mixed = 0.5 * (kstrip[end, :] + spare[pl.ds(2, 1), :])
         g1, l1 = group[0:1, :], lane[0:1, :]
         dropped = jnp.logical_or(jnp.logical_or(g1 == 2, g1 == 3),
                                  jnp.logical_or(l1 == EXTRA + 1, l1 == EXTRA + 2))
@@ -579,26 +581,6 @@
 
     row = column_sum(row)
 
-    def reduce(value, slot, recv, me, count, dev, between):
-        red[slot] = value
-        mine = pl.ds(me, 1)
-        cps = [
-            pltpu.make_async_remote_copy(
-                src_ref=red.at[slot, pl.ds(0, 1)], dst_ref=recv.at[mine],
-                send_sem=red_sem.at[2 * slot], recv_sem=red_sem.at[2 * slot + 1],
-                device_id=dev(d), device_id_type=MESH)
-            for d in range(1, count)
-        ]
-        for c in cps:
-            c.start()
-        recv[mine, :] = value[0:1, :]
-        between()
-        settle(recv.at[pl.ds(0, count - 1)], red_sem.at[2 * slot + 1])
-        out = recv[pl.ds(0, 1), :]
-        for d in range(1, count):
-            out = out + recv[pl.ds(d, 1), :]
-        return jnp.broadcast_to(out, (8, cols))
-
     outer = jnp.logical_or(lane < 3, lane > cols - 4)
 
     def close_rims(stages):
@@ -613,10 +595,25 @@
                 return carry
             lax.fori_loop(0, tiles, close, 0, unroll=split(tiles, 8))
 
-    row = reduce(row, 0, redlon, lo, lon_count,
-                 lambda d: (la, lax.rem(lo + d, lon_count)), lambda: close_rims((1, 2)))
-    row = reduce(row, 1, redlat, la, lat_count,
-                 lambda d: (lax.rem(la + d, lat_count), lo), lambda: close_rims((3,)))
+    everyone = lat_count * lon_count
+    spots = [(i, j) for i in range(lat_count) for j in range(lon_count) if i or j]
+    mine = pl.ds(la * lon_count + lo, 1)
+    red[...] = row
+    redin[mine, :] = row[0:1, :]
+    pl.semaphore_wait(known, lat_count - 1)
+    for i, j in reversed(spots):
+        pltpu.make_async_remote_copy(
+            src_ref=red.at[pl.ds(0, 1)], dst_ref=redin.at[mine],
+            send_sem=red_sem.at[0], recv_sem=red_sem.at[1],
+            device_id=(lax.rem(la + i, lat_count), lax.rem(lo + j, lon_count)),
+            device_id_type=MESH).start()
+    close_rims(range(1, ITERS + 1))
+    settle(redin.at[pl.ds(0, everyone - 1)], red_sem.at[1])
+    row = zero
+    for i in range(-(-everyone // 8)):
+        tile = redin[pl.ds(8 * i, 8), :]
+        row = row + (tile if 8 * i + 8 <= everyone else jnp.where(sub < everyone - 8 * i, tile, 0.0))
+    row = column_sum(row)
 
     m0, m1, m2, m3, m4, m5 = (
         jnp.broadcast_to(
@@ -640,8 +637,7 @@
         mix[i] = value
 
     settle(pack, send_sem.at[SIDES])
-    settle(redlon.at[pl.ds(0, lon_count - 1)], red_sem.at[0])
-    settle(redlat.at[pl.ds(0, lat_count - 1)], red_sem.at[2])
+    settle(redin.at[pl.ds(0, everyone - 1)], red_sem.at[0])
 
     @pl.when(not_last)
     def _():
@@ -708,10 +704,11 @@
             pltpu.VMEM((lon_count, folded, cols), f32),
             pltpu.VMEM((2 * ITERS, members, 8, cols), f32),
             pltpu.VMEM((2 * ITERS, 8, cols), f32),
-            pltpu.VMEM((2, 8, cols), f32),
-            pltpu.VMEM((-(-lon_count // 8) * 8, cols), f32),
-            pltpu.VMEM((-(-lat_count // 8) * 8, cols), f32),
-            dma((3,)), dma((3,)), dma((5,)), dma((3,)), dma((4,)),
+            pltpu.VMEM((8, cols), f32),
+            pltpu.VMEM((8, cols), f32),
+            pltpu.VMEM((-(-lat_count * lon_count // 8) * 8, cols), f32),
+            dma((3,)), dma((3,)), dma((6,)), dma((3,)), dma((2,)),
+            pltpu.SemaphoreType.REGULAR,
         ],
         compiler_params=pltpu.CompilerParams(
             collective_id=0, has_side_effects=True, vmem_limit_bytes=32 * 1024 * 1024),

time: 21.1 us -> 19 us (0.900)
  Pallas kernels: 20.3 us -> 18.2 us
    pallas_call x1, Pallas kernels: 19.2 us -> 17.1 us  [body(): pl.pallas_call(functools.partial(kernel, lat_count, lon_count), out_shape...]
where the time goes in v5:
time: 19 us; the launch traced here: 18.9 us
  Pallas kernels  18.2 us (96%)
  between operations  0.64 us (3%)
    pallas_call x1, Pallas kernels, body(): pl.pallas_call(functools.partial(kernel, lat_count, lon_count), out_shape...  17.1 us
    pallas_call x1, Pallas kernels, body(): pl.pallas_call(finish, out_shape=(shape, shape), in_specs=[vmem] * 4, out...  1.18 us

profile of v5, /device:TPU:0, one launch (start us, length us, event | category | flops | bytes accessed | tf_op | source)
XLA Modules:
  0.0 18.9 jit_solution(12177368024748693661)
XLA Ops:
  0.6 17.1 %shard_map.68 = (f32[15,224,128]{2,1,0:T(8,128)S(1)}, f32[3,8,224,128]{3,2,1,0:T(8,128)S(1)}, f32[7,8,128]{2,1,0:T(8,128)S(1)}, f32[192,128]{1,0:T(8,128)S(1)}) custom-call(f32[8,192,128]{2,1,0:T(8,128)} %rhs.1, f32[192,128]{1,0:T(8,128)} %center_hbm.1, f32[4,192,128]{2,1,0:T(8,128)} %coup_hbm.1, s32[192,128]{1,0:T(8,128)} %land_hbm.1, s32[8,128]{1,0:T(8,128)} %bitcast.1), custom_call_target="tpu_custom_call" | custom-call | tf_op jit(solution)/shard_map/pallas_call | solution.py:683
  17.7 1.2 %shard_map.69 = (f32[8,192,128]{2,1,0:T(8,128)}, f32[8,192,128]{2,1,0:T(8,128)}) custom-call(f32[15,224,128]{2,1,0:T(8,128)S(1)} %get-tuple-element.6.st, f32[3,8,224,128]{3,2,1,0:T(8,128)S(1)} %get-tuple-element.7.vk, f32[7,8,128]{2,1,0:T(8,128)S(1)} %get-tuple-element.8.mix, f32[192,128]{1,0:T(8,128)S(1)} %get-tuple-element.9.center), custom_call_target="tpu_custom_call" | custom-call | tf_op jit(solution)/shard_map/pallas_call | solution.py:717

commit v6 on v5

--- a/solution.py
+++ b/solution.py
@@ -25,7 +25,7 @@
 def kernel(
     lat_count, lon_count,
     rhs, center_hbm, coup_hbm, land_hbm, partner_hbm, st, vk, mix, cen,
-    land, partner, strips, kstrip, beyond, coefm, coefs, wide, pack, packin, rowin, diagin, fold,
+    land, partner, strips, kstrip, beyond, coefm, coefs, wide, pack, packin, loose, rowin, diagin, fold,
     macc, sacc, red, spare, redin,
     load_sem, send_sem, recv_sem, fold_sem, red_sem, known,
 ):
@@ -123,9 +123,36 @@
                 packs[g] = jnp.where(here, x, packs[g])
                 packs[2 + g] = jnp.where(after, x, packs[2 + g])
         for side in range(2):
-            for g in range(2):
-                pack[side, g, t] = packs[2 * side + g]
+            pack[side, 0, t] = packs[2 * side]
+            loose[side, t] = packs[2 * side + 1]
         return carry
+
+    packed = tiles // 4
+    dense = packed % 3 == 0
+    dense_count = packed // 3 * 2 if dense else packed
+    used = len(COUPLED) * SLOT
+
+    def squeeze(side):
+        if not dense:
+            for t in range(packed):
+                pack[side, 1, t] = loose[side, t]
+            return
+        for h in range(packed // 3):
+            a, b, c = (loose[side, 3 * h + i] for i in range(3))
+            pack[side, 1, 2 * h] = jnp.where(lane < used, a, roll(b, used))
+            pack[side, 1, 2 * h + 1] = jnp.where(lane < used, c, roll(b, 2 * SLOT))
+
+    def unsqueeze(side):
+        if not dense:
+            for t in range(packed):
+                loose[side, t] = packin[side, 1, t]
+            return
+        for h in range(packed // 3):
+            x, y = packin[side, 1, 2 * h], packin[side, 1, 2 * h + 1]
+            loose[side, 3 * h] = x
+            loose[side, 3 * h + 1] = jnp.where(
+                lane < 3 * SLOT, roll(x, cols - used), roll(y, cols - 2 * SLOT))
+            loose[side, 3 * h + 2] = y
 
     top, bottom = pl.ds(EDGE + rows - 3, 3), pl.ds(EDGE, 3)
 
@@ -135,8 +162,9 @@
             device_id=dev, device_id_type=MESH)
 
     def side_copies(g, landing):
-        return [remote(pack.at[0, g], packin.at[0, g], SIDES, landing, (la, east)),
-                remote(pack.at[1, g], packin.at[1, g], SIDES, landing, (la, west))]
+        part = pl.ds(0, dense_count if g else packed)
+        return [remote(pack.at[i, g, part], packin.at[i, g, part], SIDES, landing, (la, dev))
+                for i, dev in enumerate((east, west))]
     sides, sides_k = side_copies(0, SIDES), side_copies(1, SIDES_K)
     pair = pl.ds(RIM, 2)
     low, high = pl.ds(5, 3), pl.ds(0, 3)
@@ -202,6 +230,8 @@
     loads[-1].wait()
     lax.fori_loop(0, inner, prep, 0, unroll=split(inner, 11))
     lax.fori_loop(0, tiles // 4, fill, 0, unroll=split(tiles // 4, 6))
+    for side in range(2):
+        squeeze(side)
 
     @pl.when(jnp.logical_not(send_first))
     def _():
@@ -450,7 +480,7 @@
 
     def merge(g, ref):
         def step(t, carry):
-            fw, fe = packin[0, g, t], packin[1, g, t]
+            fw, fe = (loose[i, t] if g else packin[i, 0, t] for i in range(2))
             for q in range(4):
                 rs = at(first + t * 4 + q)
                 x = ref[rs, :]
@@ -460,7 +490,9 @@
                 ref[rs, :] = jnp.where(jnp.logical_and(place > 12, keep), roll(fe, 10 - 3 * q), x)
             return carry
         lax.fori_loop(0, tiles // 4, step, 0, unroll=split(tiles // 4, 6))
-    settle(packin.at[:, 1], recv_sem.at[SIDES_K])
+    settle(packin.at[:, 1, pl.ds(0, dense_count)], recv_sem.at[SIDES_K])
+    for side in range(2):
+        unsqueeze(side)
     merge(1, kstrip)
 
     def edge_spread(t, carry):
@@ -480,6 +512,8 @@
     def _():
         settle(diagin.at[pl.ds(2, 2), :, high], recv_sem.at[DOWN_CORNERS])
         take_corners(1, last + 1, sub < 3)
+
+    spread_tile(first - 1)
 
     @pl.when(lat_last)
     def _():
@@ -532,7 +566,6 @@
         kstrip[end, :] = jnp.where(dropped, 0.0, jnp.where(g1 == 1, mixed, kstrip[end, :]))
         bands(last + 1, last, last - 1)
 
-    spread_tile(first - 1)
     spread_tile(last)
     spread_tile(last + 1)
 
@@ -636,7 +669,7 @@
     for i, value in enumerate((q3 + q2 + q1, q2 + q3, q3, q0, q1, q2, q3)):
         mix[i] = value
 
-    settle(pack, send_sem.at[SIDES])
+    settle(st.at[0, pl.ds(0, 16 * (packed + dense_count))], send_sem.at[SIDES])
     settle(redin.at[pl.ds(0, everyone - 1)], red_sem.at[0])
 
     @pl.when(not_last)
@@ -699,6 +732,7 @@
             pltpu.VMEM((4, high, cols), f32),
             pltpu.VMEM((2, 2, tiles // 4, 8, cols), f32),
             pltpu.VMEM((2, 2, tiles // 4, 8, cols), f32),
+            pltpu.VMEM((2, tiles // 4, 8, cols), f32),
             pltpu.VMEM((2, ARRAYS, 8, cols), f32),
             pltpu.VMEM((4, 2, 8, cols), f32),
             pltpu.VMEM((lon_count, folded, cols), f32),

time: 19 us -> 19.1 us (level)
  no operation moved by 1% of the time
where the time goes in v6:
time: 19.1 us; the launch traced here: 19 us
  Pallas kernels  18.3 us (96%)
  between operations  0.64 us (3%)
    pallas_call x1, Pallas kernels, body(): pl.pallas_call(functools.partial(kernel, lat_count, lon_count), out_shape...  17.1 us
    pallas_call x1, Pallas kernels, body(): pl.pallas_call(finish, out_shape=(shape, shape), in_specs=[vmem] * 4, out...  1.18 us

profile of v6, /device:TPU:0, one launch (start us, length us, event | category | flops | bytes accessed | tf_op | source)
XLA Modules:
  0.0 19.0 jit_solution(4746281146948879354)
XLA Ops:
  0.6 17.1 %shard_map.68 = (f32[15,224,128]{2,1,0:T(8,128)S(1)}, f32[3,8,224,128]{3,2,1,0:T(8,128)S(1)}, f32[7,8,128]{2,1,0:T(8,128)S(1)}, f32[192,128]{1,0:T(8,128)S(1)}) custom-call(f32[8,192,128]{2,1,0:T(8,128)} %rhs.1, f32[192,128]{1,0:T(8,128)} %center_hbm.1, f32[4,192,128]{2,1,0:T(8,128)} %coup_hbm.1, s32[192,128]{1,0:T(8,128)} %land_hbm.1, s32[8,128]{1,0:T(8,128)} %bitcast.1), custom_call_target="tpu_custom_call" | custom-call | tf_op jit(solution)/shard_map/pallas_call | solution.py:716
  17.8 1.2 %shard_map.69 = (f32[8,192,128]{2,1,0:T(8,128)}, f32[8,192,128]{2,1,0:T(8,128)}) custom-call(f32[15,224,128]{2,1,0:T(8,128)S(1)} %get-tuple-element.6.st, f32[3,8,224,128]{3,2,1,0:T(8,128)S(1)} %get-tuple-element.7.vk, f32[7,8,128]{2,1,0:T(8,128)S(1)} %get-tuple-element.8.mix, f32[192,128]{1,0:T(8,128)S(1)} %get-tuple-element.9.center), custom_call_target="tpu_custom_call" | custom-call | tf_op jit(solution)/shard_map/pallas_call | solution.py:751
